TPU v7x, 32 devices: a whole 2x2x4 slice. The times are simulated.
32 devices in a mesh: sub: 4 (over y, x), dev: 8 (over z, core).
Axes of the slice: x: 2, y: 2, z: 4, core: 2. Of those that a mesh axis runs over, the one named last changes fastest.
Arguments:
- child_tiles: float32 [8192, 128, 128], P(('sub', 'dev')), parts along dimension 0, may hold values from -6 to 6
- l_slab: float32 [32768, 512], P(('sub', 'dev')), parts along dimension 0, may hold values from -6 to 6
- u_slab: float32 [512, 131072], P(None, ('sub', 'dev')), parts along dimension 1, may hold values from -0.25 to 0.25
- parent_own_entries: float32 [9216, 128, 128], P(('sub', 'dev')), parts along dimension 0, may hold values from -6 to 6
- parent_label: int32 [8, 32], P('sub'), parts along dimension 0, may hold values from 0 to 47, as said below
Outputs:
- parent_front: float32 [9216, 128, 128], P(('sub', 'dev')), parts along dimension 0
There are 4 independent parts, one for each index of `sub`. A program takes and returns all parts, laid end to end along the dimension named above; each array names one. Nothing has to cross between parts.
Inputs may be any that keep to these rules, and one draw needn't show every extreme that they name: `parent_label`: the 32 labels of one child are distinct. For child c and tile row k, the label modulo 8 is sigma((k mod 8 + k // 8 + 4 c) mod 8), with sigma a permutation of 0 to 7 common to both children.
All inputs are finite; a program needn't handle non-finite values.
Results may differ from a plain program's by a relative error of at most 0.000051.
Values sent between devices are 32-bit elements; how exact they have to be, the bound alone decides.
No kernel may reach another device: no remote copies, remote signals or barrier semaphores. Data moves between devices by JAX's collectives and lax.ppermute only.
A program may use at most 128 MiB of HBM per device.

v0:
```python
import jax
import jax.numpy as jnp
from jax import lax
from jax.sharding import PartitionSpec as P

TILE_EDGE = 128
MT = 32
PT = 48
CGR = 4
PR = 8


def tile_targets(labels, count, ndev, me_index):
    cgc = ndev // 8
    pcols = ndev // 8
    ncd = ndev // 2
    cols_loc = MT // cgc
    inner = me_index % ncd
    local = jnp.arange(count, dtype=jnp.int32)
    tile_row = inner // cgc + CGR * (local // cols_loc)
    tile_col = inner % cgc + cgc * (local % cols_loc)
    columns = jnp.arange(MT, dtype=jnp.int32)
    label_row = jnp.sum(
        jnp.where(tile_row[:, None] == columns[None, :], labels[None, :], 0), axis=1
    )
    label_col = jnp.sum(
        jnp.where(tile_col[:, None] == columns[None, :], labels[None, :], 0), axis=1
    )
    dest_dev = label_row % PR * pcols + label_col % pcols
    dest_slot = label_row // PR * (PT // pcols) + label_col // pcols
    return (dest_dev, dest_slot)


def update_tiles(child_part, left_rows, u_slab, cols_loc):
    product = jnp.dot(
        left_rows, u_slab, precision=lax.Precision.HIGHEST, preferred_element_type=jnp.float32
    )
    row_tiles = left_rows.shape[0] // TILE_EDGE
    product = (
        product.reshape(row_tiles, TILE_EDGE, cols_loc, TILE_EDGE)
        .transpose(0, 2, 1, 3)
        .reshape(row_tiles * cols_loc, TILE_EDGE, TILE_EDGE)
    )
    return child_part - product


def pack_tiles(updated, dest_dev, dest_slot, ndev, bound):
    count = updated.shape[0]
    order = jnp.arange(count, dtype=jnp.int32)
    earlier = order[None, :] < order[:, None]
    same_dest = dest_dev[:, None] == dest_dev[None, :]
    arrival = jnp.sum(jnp.where(same_dest & earlier, 1, 0), axis=1).astype(jnp.int32)
    position = dest_dev * bound + arrival
    places = jnp.arange(ndev * bound, dtype=jnp.int32)
    hits = places[:, None] == position[None, :]
    select = hits.astype(jnp.float32)
    packed = jnp.dot(
        select,
        updated.reshape(count, -1),
        precision=lax.Precision.HIGHEST,
        preferred_element_type=jnp.float32,
    )
    filled = jnp.sum(jnp.where(hits, 1, 0), axis=1)
    sent_slot = jnp.where(filled > 0, jnp.sum(jnp.where(hits, dest_slot[None, :], 0), axis=1), -1)
    return (packed.reshape(ndev, bound, -1), sent_slot.reshape(ndev, bound))


def assemble_front(incoming_tiles, incoming_slot, slot_count):
    flat = incoming_tiles.reshape(-1, incoming_tiles.shape[-1])
    select = (
        jnp.arange(slot_count, dtype=jnp.int32)[:, None] == incoming_slot.reshape(-1)[None, :]
    ).astype(jnp.float32)
    return jnp.dot(
        select, flat, precision=lax.Precision.HIGHEST, preferred_element_type=jnp.float32
    )


def body(child_tiles, l_slab, u_slab, parent_own_entries, parent_label):
    ndev = lax.axis_size("dev")
    me_index = lax.axis_index("dev")
    cgc = ndev // 8
    pcols = ndev // 8
    bound = max(1, MT // (cgc * pcols))
    cols_loc = MT // cgc
    tiles_dev = child_tiles.shape[0]
    slot_count = parent_own_entries.shape[0]
    child_id = me_index // (ndev // 2)
    labels = lax.dynamic_index_in_dim(parent_label, child_id, 0, keepdims=False)
    updated = update_tiles(child_tiles, l_slab, u_slab, cols_loc)
    dest_dev, dest_slot = tile_targets(labels, tiles_dev, ndev, me_index)
    packed, sent_slot = pack_tiles(updated, dest_dev, dest_slot, ndev, bound)
    incoming_tiles, incoming_slot = (
        lax.all_to_all(packed, "dev", split_axis=0, concat_axis=0, tiled=True),
        lax.all_to_all(sent_slot, "dev", split_axis=0, concat_axis=0, tiled=True),
    )
    summed_entries = assemble_front(incoming_tiles, incoming_slot, slot_count)
    return parent_own_entries + summed_entries.reshape(slot_count, TILE_EDGE, TILE_EDGE)


def solution(mesh):
    in_specs = (
        P(("sub", "dev"), None, None),
        P(("sub", "dev"), None),
        P(None, ("sub", "dev")),
        P(("sub", "dev"), None, None),
        P("sub", None),
    )
    out_specs = P(("sub", "dev"), None, None)
    return jax.shard_map(body, mesh=mesh, in_specs=in_specs, out_specs=out_specs, check_vma=False)
```

profile of v0, /device:TPU:0, one launch (start us, length us, event | category | flops | bytes accessed | tf_op | source)
XLA Modules:
  0.0 551.1 jit_solution(3916465375924862741)
XLA Ops:
  0.0 0.0 copy-start
  0.0 0.8 dynamic-slice_bitcast_fusion
  0.8 0.1 select_reduce_fusion.3
  0.9 0.2 select_reduce_fusion.2
  1.1 0.2 select_reduce_fusion.1
  1.3 0.7 select_n.112
  2.0 6.4 %all-to-all-start = ((s32[8,1,32]{2,1,0:T(1,128)}), s32[8,1,32]{2,1,0:T(1,128)S(1)}, u32[]{:S(2)}, u32[]{:S(2)}) async-start(s32[8,1,32]{2,1,0:T(1,128)} %select_n.112), calls=%async_computation | async-start | bytes 8192 | tf_op jit(solution)/shard_map/all_to_all | solution.py:94
  8.4 0.0 copy-done
  8.4 29.1 %convolution_bitcast_fusion = f32[128,8,32,128]{3,1,2,0:T(8,128)S(1)} fusion(f32[1024,512]{1,0:T(8,128)S(1)} %copy-done, f32[512,4096]{1,0:T(8,128)} %param.7), kind=kOutput, calls=%fused_computation.3 | convolution fusion | flops 25769803776 | bytes 27262976 | tf_op jit(solution)/shard_map/dot_general | solution.py:35
  37.5 3.6 copy.14
  41.1 6.4 %bitcast_bitcast_fusion = f32[8,32,128,128]{3,1,2,0:T(8,128)} fusion(f32[8,128,32,128]{3,2,1,0:T(8,128)S(1)} %bitcast.24), kind=kLoop, calls=%fused_computation.1 | loop fusion | bytes 33554432 | tf_op jit(solution)/shard_map/transpose | solution.py:41
  47.5 15.2 %copy.10 = f32[8,32,128,128]{3,2,1,0:T(8,128)S(1)} copy(f32[8,32,128,128]{3,1,2,0:T(8,128)} %bitcast_bitcast_fusion) | data formatting | bytes 33554432 | tf_op jit(solution)/shard_map/transpose | solution.py:41
  62.7 12.9 %bitcast_subtract_fusion = f32[256,128,128]{2,1,0:T(8,128)} fusion(f32[256,128,128]{2,1,0:T(8,128)} %param.5, f32[8,32,128,128]{3,2,1,0:T(8,128)S(1)} %copy.10), kind=kLoop, calls=%fused_computation.2 | loop fusion | flops 4194304 | bytes 50331648 | tf_op jit(solution)/shard_map/sub | solution.py:44
  75.6 18.2 %reshape.148 = f32[256,16384,1]{1,0,2:T(8,128)} reshape(f32[256,128,128]{2,1,0:T(8,128)} %bitcast_subtract_fusion) | data formatting | bytes 33554432 | tf_op jit(solution)/shard_map/reshape | solution.py:59
  93.8 16.0 %fusion.3 = f32[8,32,16384]{2,1,0:T(8,128)} fusion(f32[256,16384,1]{1,0,2:T(8,128)} %reshape.148, s32[256]{0:T(256)S(1)} %multiply_add_fusion.2, s32[8,32]{1,0:T(8,128)S(1)} %multiply_add_fusion), kind=kOutput, calls=%fused_computation.12 | convolution fusion | flops 12884967424 | bytes 33556480 | tf_op jit(solution)/shard_map/dot_general | solution.py:57
  109.8 0.0 all-to-all-done
  109.8 5.8 %all-to-all-start.1 = ((f32[8,32,16384]{2,1,0:T(8,128)}), f32[8,32,16384]{2,1,0:T(8,128)}, u32[]{:S(2)}, u32[]{:S(2)}) async-start(f32[8,32,16384]{2,1,0:T(8,128)} %fusion.3), calls=%async_computation.1 | async-start | bytes 33554432 | tf_op jit(solution)/shard_map/all_to_all | solution.py:93
  115.6 0.5 broadcast.249
  116.1 0.6 reduce.3
  116.7 0.1 eq.107
  116.8 362.5 %all-to-all-done.1 = f32[8,32,16384]{2,1,0:T(8,128)} async-done(((f32[8,32,16384]{2,1,0:T(8,128)}), f32[8,32,16384]{2,1,0:T(8,128)}, u32[]{:S(2)}, u32[]{:S(2)}) %all-to-all-start.1) | async-done | bytes 16777248 | tf_op jit(solution)/shard_map/all_to_all | solution.py:93
  479.2 17.4 %copy.11 = f32[16384,256]{1,0:T(8,128)} copy(f32[16384,256]{0,1:T(8,128)} %bitcast.5) | data formatting | bytes 33554432 | tf_op jit(solution)/shard_map/dot_general | solution.py:73
  496.7 0.0 copy-start.1
  496.7 37.6 %copy_add_fusion = f32[288,128,128]{2,0,1:T(8,128)} fusion(f32[288,128,128]{2,1,0:T(8,128)} %param.8, f32[128,128,256]{2,1,0:T(8,128)} %bitcast.23, s32[256]{0:T(256)S(1)} %eq.107), kind=kOutput, calls=%fused_computation | convolution fusion | flops 14500306944 | bytes 54526976 | tf_op jit(solution)/shard_map/dot_general | solution.py:73
  534.2 16.9 %copy.13 = f32[288,128,128]{2,1,0:T(8,128)} copy(f32[288,128,128]{2,0,1:T(8,128)} %copy_add_fusion) | data formatting | bytes 37748736 | tf_op jit(solution)/shard_map/add | solution.py:97
  551.1 0.0 copy-done.1
  (5 shorter events, 0.0 us)
Async XLA Ops:
  0.0 8.4 %copy-start = (f32[1024,512]{1,0:T(8,128)S(1)}, f32[1024,512]{1,0:T(8,128)}, u32[]{:S(2)}) copy-start(f32[1024,512]{1,0:T(8,128)} %param.6) | copy-start | bytes 6291460
  2.0 107.8 %all-to-all-start = ((s32[8,1,32]{2,1,0:T(1,128)}), s32[8,1,32]{2,1,0:T(1,128)S(1)}, u32[]{:S(2)}, u32[]{:S(2)}) async-start(s32[8,1,32]{2,1,0:T(1,128)} %select_n.112), calls=%async_computation | async-start | bytes 8192 | tf_op jit(solution)/shard_map/all_to_all | solution.py:94
  109.8 369.4 %all-to-all-start.1 = ((f32[8,32,16384]{2,1,0:T(8,128)}), f32[8,32,16384]{2,1,0:T(8,128)}, u32[]{:S(2)}, u32[]{:S(2)}) async-start(f32[8,32,16384]{2,1,0:T(8,128)} %fusion.3), calls=%async_computation.1 | async-start | bytes 33554432 | tf_op jit(solution)/shard_map/all_to_all | solution.py:93
  496.7 54.5 %copy-start.1 = (f32[1024,512]{1,0:T(8,128)S(1)}, f32[1024,512]{1,0:T(8,128)}, u32[]{:S(2)}) copy-start(f32[1024,512]{1,0:T(8,128)} %param.6) | copy-start | bytes 6291460
where the time goes:
time: 552 us; the launch traced here: 551 us
  waiting for transfers between devices  362 us (66%)
  matrix products  82.7 us (15%)
  local copies, waits for them, and re-layouts  79.9 us (14%)
  other arithmetic  13.9 us (3%)
  starting transfers between devices  12.1 us (2%)
    all_to_all x1, waiting for transfers between devices, body(): lax.all_to_all(packed, 'dev', split_axis=0, concat_axis=0, tiled=True)  362 us
    dot_general x1, matrix products, assemble_front(): jnp.dot(select, flat, precision=lax.Precision.HIGHEST, preferred_element_...  37.6 us
    dot_general x1, matrix products, update_tiles(): jnp.dot(left_rows, u_slab, precision=lax.Precision.HIGHEST, preferred_ele...  29.1 us
    transpose x2, local copies, waits for them, and re-layouts, update_tiles(): product = product.reshape(row_tiles, TILE_EDGE, cols_loc, TILE_EDGE).tran...  21.6 us
    reshape x1, local copies, waits for them, and re-layouts, pack_tiles(): updated.reshape(count, -1)  18.2 us
    dot_general x1, local copies, waits for them, and re-layouts, assemble_front(): jnp.dot(select, flat, precision=lax.Precision.HIGHEST, preferred_element_...  17.4 us
    add x1, local copies, waits for them, and re-layouts, body(): parent_own_entries + summed_entries.reshape(slot_count, TILE_EDGE, TILE_E...  16.9 us
    dot_general x1, matrix products, pack_tiles(): jnp.dot(select, updated.reshape(count, -1), precision=lax.Precision.HIGHE...  16 us
  transfers between devices with their start and end apart: 2, of which 1 were waited for; matrix products, arithmetic and copies ran while one was open for 19% of the time, Pallas kernels for 0%

commit v1 on v0

--- a/solution.py
+++ b/solution.py
@@ -1,13 +1,271 @@
+import functools
+
 import jax
 import jax.numpy as jnp
 from jax import lax
+from jax.experimental import pallas as pl
+from jax.experimental.pallas import tpu as pltpu
 from jax.sharding import PartitionSpec as P
+
 
 TILE_EDGE = 128
 MT = 32
 PT = 48
 CGR = 4
 PR = 8
+
+
+def row_for(labels, me, ncd, dest):
+    child, inner = me // ncd, me % ncd
+    row = jnp.int32(0)
+    for t in range(MT // CGR):
+        row = jnp.where(labels[child, inner + CGR * t] % PR == dest, t, row)
+    return row
+
+
+def parent_row(labels, me, ncd, source):
+    child, inner = source // ncd, source % ncd
+    row = jnp.int32(0)
+    for t in range(MT // CGR):
+        label = labels[child, inner + CGR * t]
+        row = jnp.where(label % PR == me, label // PR, row)
+    return row
+
+
+def stripe_kernel(labels, me, left, right, child, after, out):
+    product = jnp.dot(
+        left[...], right[...], precision=lax.Precision.HIGHEST, preferred_element_type=jnp.float32
+    )
+    for g in range(out.shape[0]):
+        out[g] = child[g] - product[:, g * TILE_EDGE : (g + 1) * TILE_EDGE]
+
+
+def stripe(labels, me, l_slab, u_slab, child_tiles, after, ncd, step, first, count, group):
+    panel = l_slab.shape[1]
+    groups = MT // group
+
+    def row(lab, who):
+        return row_for(lab, who[0], ncd, who[0] ^ step)
+
+    grid_spec = pltpu.PrefetchScalarGridSpec(
+        num_scalar_prefetch=2,
+        grid=(count // group,),
+        in_specs=[
+            pl.BlockSpec((TILE_EDGE, panel), lambda j, lab, who: (row(lab, who), 0)),
+            pl.BlockSpec((panel, group * TILE_EDGE), lambda j, lab, who: (0, first // group + j)),
+            pl.BlockSpec(
+                (group, TILE_EDGE, TILE_EDGE),
+                lambda j, lab, who: (row(lab, who) * groups + first // group + j, 0, 0),
+            ),
+            pl.BlockSpec(memory_space=pl.ANY),
+        ],
+        out_specs=pl.BlockSpec((group, TILE_EDGE, TILE_EDGE), lambda j, lab, who: (j, 0, 0)),
+    )
+    tile = TILE_EDGE * TILE_EDGE
+    return pl.pallas_call(
+        stripe_kernel,
+        grid_spec=grid_spec,
+        out_shape=jax.ShapeDtypeStruct((count, TILE_EDGE, TILE_EDGE), jnp.float32),
+        cost_estimate=pl.CostEstimate(
+            flops=2 * 6 * count * tile * panel,
+            bytes_accessed=4 * (2 * count * tile + TILE_EDGE * panel * (1 + count)),
+            transcendentals=0,
+        ),
+    )(labels, me, l_slab, u_slab, child_tiles, after)
+
+
+def start_front_kernel(ncd, labels, me, own, tiles, out):
+    out[...] = own[...]
+
+    @pl.when(pl.program_id(0) == parent_row(labels, me[0], ncd, me[0]))
+    def _():
+        def add(j, carry):
+            at = labels[me[0] // ncd, j]
+            out[at] = out[at] + tiles[j]
+            return carry
+
+        lax.fori_loop(0, MT, add, 0)
+
+
+def start_front(labels, me, own, tiles, ncd):
+    block = (PT, TILE_EDGE, TILE_EDGE)
+    grid_spec = pltpu.PrefetchScalarGridSpec(
+        num_scalar_prefetch=2,
+        grid=(own.shape[0] // PT,),
+        in_specs=[
+            pl.BlockSpec(block, lambda q, lab, who: (q, 0, 0)),
+            pl.BlockSpec(tiles.shape, lambda q, lab, who: (0, 0, 0)),
+        ],
+        out_specs=pl.BlockSpec(block, lambda q, lab, who: (q, 0, 0)),
+    )
+    return pl.pallas_call(
+        functools.partial(start_front_kernel, ncd),
+        grid_spec=grid_spec,
+        out_shape=jax.ShapeDtypeStruct(own.shape, own.dtype),
+        name="start_front",
+    )(labels, me, own, tiles)
+
+
+def each(count, action):
+    def one(i, carry):
+        action(i)
+        return carry
+
+    lax.fori_loop(0, count, one, 0)
+
+
+def extend_kernel(ncd, step, first, labels, me, tiles, front_in, front, sums, fetched, stored):
+    source = me[0] ^ step
+    base = parent_row(labels, me[0], ncd, source) * PT
+    child = source // ncd
+    count = tiles.shape[0]
+
+    def slot(i):
+        return front.at[base + labels[child, first + i]]
+
+    def fetch(i):
+        return pltpu.make_async_copy(slot(i), sums.at[i], fetched.at[i])
+
+    def store(i):
+        return pltpu.make_async_copy(sums.at[i], slot(i), stored.at[i])
+
+    def add(i):
+        fetch(i).wait()
+        sums[i] = sums[i] + tiles[i]
+        store(i).start()
+
+    each(count, lambda i: fetch(i).start())
+    each(count, add)
+    each(count, lambda i: store(i).wait())
+
+
+def extend(labels, me, tiles, front, ncd, step, first):
+    count = tiles.shape[0]
+    grid_spec = pltpu.PrefetchScalarGridSpec(
+        num_scalar_prefetch=2,
+        grid=(1,),
+        in_specs=[
+            pl.BlockSpec(tiles.shape, lambda i, lab, who: (0, 0, 0)),
+            pl.BlockSpec(memory_space=pl.ANY),
+        ],
+        out_specs=pl.BlockSpec(memory_space=pl.ANY),
+        scratch_shapes=[
+            pltpu.VMEM(tiles.shape, jnp.float32),
+            pltpu.SemaphoreType.DMA((count,)),
+            pltpu.SemaphoreType.DMA((count,)),
+        ],
+    )
+    return pl.pallas_call(
+        functools.partial(extend_kernel, ncd, step, first),
+        grid_spec=grid_spec,
+        out_shape=jax.ShapeDtypeStruct(front.shape, front.dtype),
+        input_output_aliases={3: 0},
+    )(labels, me, tiles, front)
+
+
+def take_kernel(ncd, step, first, labels, me, front, out, fetched):
+    source = me[0] ^ step
+    base = parent_row(labels, me[0], ncd, source) * PT
+    child = source // ncd
+
+    def fetch(i):
+        slot = base + labels[child, first + i]
+        return pltpu.make_async_copy(front.at[slot], out.at[i], fetched.at[i])
+
+    each(out.shape[0], lambda i: fetch(i).start())
+    each(out.shape[0], lambda i: fetch(i).wait())
+
+
+def put_kernel(ncd, step, first, labels, me, tiles, old, front_in, front, sums, stored):
+    source = me[0] ^ step
+    base = parent_row(labels, me[0], ncd, source) * PT
+    child = source // ncd
+
+    def store(i):
+        slot = base + labels[child, first + i]
+        return pltpu.make_async_copy(sums.at[i], front.at[slot], stored.at[i])
+
+    def add(i):
+        sums[i] = old[i] + tiles[i]
+        store(i).start()
+
+    each(tiles.shape[0], add)
+    each(tiles.shape[0], lambda i: store(i).wait())
+
+
+def take(labels, me, front, ncd, step, first, count):
+    shape = (count, TILE_EDGE, TILE_EDGE)
+    grid_spec = pltpu.PrefetchScalarGridSpec(
+        num_scalar_prefetch=2,
+        grid=(1,),
+        in_specs=[pl.BlockSpec(memory_space=pl.ANY)],
+        out_specs=pl.BlockSpec(shape, lambda i, lab, who: (0, 0, 0)),
+        scratch_shapes=[pltpu.SemaphoreType.DMA((count,))],
+    )
+    return pl.pallas_call(
+        functools.partial(take_kernel, ncd, step, first),
+        grid_spec=grid_spec,
+        out_shape=jax.ShapeDtypeStruct(shape, jnp.float32),
+    )(labels, me, front)
+
+
+def put(labels, me, tiles, old, front, ncd, step, first):
+    block = pl.BlockSpec(tiles.shape, lambda i, lab, who: (0, 0, 0))
+    grid_spec = pltpu.PrefetchScalarGridSpec(
+        num_scalar_prefetch=2,
+        grid=(1,),
+        in_specs=[block, block, pl.BlockSpec(memory_space=pl.ANY)],
+        out_specs=pl.BlockSpec(memory_space=pl.ANY),
+        scratch_shapes=[
+            pltpu.VMEM(tiles.shape, jnp.float32),
+            pltpu.SemaphoreType.DMA((tiles.shape[0],)),
+        ],
+    )
+    return pl.pallas_call(
+        functools.partial(put_kernel, ncd, step, first),
+        grid_spec=grid_spec,
+        out_shape=jax.ShapeDtypeStruct(front.shape, front.dtype),
+        input_output_aliases={4: 0},
+    )(labels, me, tiles, old, front)
+
+
+SENDS = (
+    (6, 0, 4, 4),
+    (6, 4, 28, 4),
+    (4, 0, 32, 8),
+    (7, 0, 32, 8),
+    (5, 0, 16, 8),
+    (5, 16, 12, 4),
+    (5, 28, 4, 4),
+    (1, 0, 32, 8),
+    (2, 0, 32, 8),
+    (3, 0, 32, 8),
+)
+ADDS = ((1, 0), (6, 0), (6, 4), (2, 0), (3, 0), (7, 0), (4, 0), (5, 0), (5, 16))
+LAST = (5, 28)
+
+
+def body_rows(child_tiles, l_slab, u_slab, parent_own_entries, parent_label):
+    ndev = lax.axis_size("dev")
+    ncd = ndev // 2
+    me = lax.axis_index("dev").astype(jnp.int32).reshape(1)
+    arrived = {}
+    after = parent_label
+    for step, first, count, group in SENDS:
+        tiles = stripe(
+            parent_label, me, l_slab, u_slab, child_tiles, after, ncd, step, first, count, group
+        )
+        after = tiles
+        pairs = [(d, d ^ step) for d in range(ndev)]
+        arrived[step, first] = lax.ppermute(tiles, "dev", pairs)
+    kept = stripe(parent_label, me, l_slab, u_slab, child_tiles, after, ncd, 0, 0, MT, 8)
+    front = start_front(parent_label, me, parent_own_entries, kept, ncd)
+    for step, first in ADDS:
+        front = extend(parent_label, me, arrived[step, first], front, ncd, step, first)
+    step, first = LAST
+    tiles = arrived[step, first]
+    old = take(parent_label, me, front, ncd, step, first, tiles.shape[0])
+    return put(parent_label, me, tiles, old, front, ncd, step, first)
 
 
 def tile_targets(labels, count, ndev, me_index):
@@ -75,7 +333,7 @@
     )
 
 
-def body(child_tiles, l_slab, u_slab, parent_own_entries, parent_label):
+def body_grid(child_tiles, l_slab, u_slab, parent_own_entries, parent_label):
     ndev = lax.axis_size("dev")
     me_index = lax.axis_index("dev")
     cgc = ndev // 8
@@ -106,4 +364,6 @@
         P("sub", None),
     )
     out_specs = P(("sub", "dev"), None, None)
+    rows_only = mesh.shape["dev"] == PR
+    body = body_rows if rows_only else body_grid
     return jax.shard_map(body, mesh=mesh, in_specs=in_specs, out_specs=out_specs, check_vma=False)

time: 552 us -> 411 us (0.74)
  Pallas kernels: 0 us -> 144 us
  waiting for transfers between devices: 362 us -> 247 us
  matrix products: 82.7 us -> 0 us
  local copies, waits for them, and re-layouts: 79.9 us -> 1.32 us
  other arithmetic: 13.9 us -> 0 us
    all_to_all x2 -> x0, waiting for transfers between devices: 362 us -> none  [the longest x1 362 us: body(): lax.all_to_all(packed, 'dev', split_axis=0, concat_axis=0, tiled=True)]
    ppermute x0 -> x10, waiting for transfers between devices: none -> 247 us  [body_rows(): arrived[step, first] = lax.ppermute(tiles, 'dev', pairs)]
    pallas_call x0 -> x23, Pallas kernels: none -> 144 us  [the longest x11 82 us: stripe(): pl.pallas_call(stripe_kernel, grid_spec=grid_spec, out_shape=jax.ShapeDty...]
    dot_general x3 -> x0, matrix products: 82.7 us -> none  [the longest x1 37.6 us: assemble_front(): jnp.dot(select, flat, precision=lax.Precision.HIGHEST, preferred_element_...]
    transpose x2 -> x0, local copies, waits for them, and re-layouts: 21.6 us -> none  [update_tiles(): product = product.reshape(row_tiles, TILE_EDGE, cols_loc, TILE_EDGE).tran...]
    reshape x1 -> x0, local copies, waits for them, and re-layouts: 18.2 us -> none  [pack_tiles(): updated.reshape(count, -1)]
    dot_general x1 -> x0, local copies, waits for them, and re-layouts: 17.4 us -> none  [assemble_front(): jnp.dot(select, flat, precision=lax.Precision.HIGHEST, preferred_element_...]
    add x1 -> x0, local copies, waits for them, and re-layouts: 16.9 us -> none  [body(): parent_own_entries + summed_entries.reshape(slot_count, TILE_EDGE, TILE_E...]
  transfers between devices with their start and end apart: 2 -> 10, of which waited for: 1 -> 4; matrix products, arithmetic and copies ran while one was open for 19% -> 0% of each run, Pallas kernels for 0% -> 31%
where the time goes in v1:
time: 411 us; the launch traced here: 408 us
  waiting for transfers between devices  247 us (60%)
  Pallas kernels  144 us (35%)
  starting transfers between devices  15 us (4%)
    ppermute x10, waiting for transfers between devices, body_rows(): arrived[step, first] = lax.ppermute(tiles, 'dev', pairs)  247 us
    pallas_call x11, Pallas kernels, stripe(): pl.pallas_call(stripe_kernel, grid_spec=grid_spec, out_shape=jax.ShapeDty...  82 us
    pallas_call x9, Pallas kernels, extend(): pl.pallas_call(functools.partial(extend_kernel, ncd, step, first), grid_s...  41.3 us
    pallas_call x1, Pallas kernels, start_front(): pl.pallas_call(functools.partial(start_front_kernel, ncd), grid_spec=grid...  16 us
    ppermute x10, starting transfers between devices, body_rows(): arrived[step, first] = lax.ppermute(tiles, 'dev', pairs)  15 us
  transfers between devices with their start and end apart: 10, of which 4 were waited for; matrix products, arithmetic and copies ran while one was open for 0% of the time, Pallas kernels for 31%

profile of v1, /device:TPU:0, one launch (start us, length us, event | category | flops | bytes accessed | tf_op | source)
XLA Modules:
  0.0 408.3 jit_solution(7756772894872862852)
XLA Ops:
  0.0 3.4 shard_map.55.after
  3.4 9.9 %shard_map.56.after = f32[28,128,128]{2,1,0:T(8,128)} custom-call(s32[2,32]{1,0:T(2,128)} %labels.45, s32[1]{0:T(128)} %bitcast.me, f32[1024,512]{1,0:T(8,128)} %left.21, f32[512,4096]{1,0:T(8,128)} %right.21, f32[256,128,128]{2,1,0:T(8,128)} %child.21, f32[4,128,128]{2,1,0:T(8,128)} %shard_map.55.after), custom_call_target="tpu_custom_call" | custom-call | flops 2818572288 | bytes 11272192 | tf_op jit(solution)/shard_map/pallas_call | solution.py:65
  13.3 5.1 %collective-permute-start.7 = (f32[28,128,128]{2,1,0:T(8,128)}, f32[28,128,128]{2,1,0:T(8,128)}, u32[]{:S(2)}, u32[]{:S(2)}) collective-permute-start(f32[28,128,128]{2,1,0:T(8,128)} %shard_map.56.after), channel_id=1, source_target_pairs={{0,6},{1,7},{2,4},{3,5},{4,2},{5,3},{6,0},{7,1},{8,14},{9,15},{10,... | collective-permute-start | bytes 5505032 | tf_op jit(solution)/shard_map/ppermute | solution.py:260
  18.4 8.9 %shard_map.57.after = f32[32,128,128]{2,1,0:T(8,128)} custom-call(s32[2,32]{1,0:T(2,128)} %labels.45, s32[1]{0:T(128)} %bitcast.me, f32[1024,512]{1,0:T(8,128)} %left.21, f32[512,4096]{1,0:T(8,128)} %right.21, f32[256,128,128]{2,1,0:T(8,128)} %child.21, f32[28,128,128]{2,1,0:T(8,128)} %shard_map.56.after), custom_call_target="tpu_custom_call" | custom-call | flops 3221225472 | bytes 12845056 | tf_op jit(solution)/shard_map/pallas_call | solution.py:65
  27.3 8.9 %shard_map.58.after = f32[32,128,128]{2,1,0:T(8,128)} custom-call(s32[2,32]{1,0:T(2,128)} %labels.45, s32[1]{0:T(128)} %bitcast.me, f32[1024,512]{1,0:T(8,128)} %left.21, f32[512,4096]{1,0:T(8,128)} %right.21, f32[256,128,128]{2,1,0:T(8,128)} %child.21, f32[32,128,128]{2,1,0:T(8,128)} %shard_map.57.after), custom_call_target="tpu_custom_call" | custom-call | flops 3221225472 | bytes 12845056 | tf_op jit(solution)/shard_map/pallas_call | solution.py:65
  36.2 5.8 %shard_map.59.after = f32[16,128,128]{2,1,0:T(8,128)} custom-call(s32[2,32]{1,0:T(2,128)} %labels.45, s32[1]{0:T(128)} %bitcast.me, f32[1024,512]{1,0:T(8,128)} %left.21, f32[512,4096]{1,0:T(8,128)} %right.21, f32[256,128,128]{2,1,0:T(8,128)} %child.21, f32[32,128,128]{2,1,0:T(8,128)} %shard_map.58.after), custom_call_target="tpu_custom_call" | custom-call | flops 1610612736 | bytes 6553600 | tf_op jit(solution)/shard_map/pallas_call | solution.py:65
  42.0 5.7 %shard_map.60.after = f32[12,128,128]{2,1,0:T(8,128)} custom-call(s32[2,32]{1,0:T(2,128)} %labels.45, s32[1]{0:T(128)} %bitcast.me, f32[1024,512]{1,0:T(8,128)} %left.21, f32[512,4096]{1,0:T(8,128)} %right.21, f32[256,128,128]{2,1,0:T(8,128)} %child.21, f32[16,128,128]{2,1,0:T(8,128)} %shard_map.59.after), custom_call_target="tpu_custom_call" | custom-call | flops 1207959552 | bytes 4980736 | tf_op jit(solution)/shard_map/pallas_call | solution.py:65
  47.7 3.4 shard_map.61.after
  51.1 8.9 %shard_map.62.after = f32[32,128,128]{2,1,0:T(8,128)} custom-call(s32[2,32]{1,0:T(2,128)} %labels.45, s32[1]{0:T(128)} %bitcast.me, f32[1024,512]{1,0:T(8,128)} %left.21, f32[512,4096]{1,0:T(8,128)} %right.21, f32[256,128,128]{2,1,0:T(8,128)} %child.21, f32[4,128,128]{2,1,0:T(8,128)} %shard_map.61.after), custom_call_target="tpu_custom_call" | custom-call | flops 3221225472 | bytes 12845056 | tf_op jit(solution)/shard_map/pallas_call | solution.py:65
  60.0 8.9 %shard_map.63.after = f32[32,128,128]{2,1,0:T(8,128)} custom-call(s32[2,32]{1,0:T(2,128)} %labels.45, s32[1]{0:T(128)} %bitcast.me, f32[1024,512]{1,0:T(8,128)} %left.21, f32[512,4096]{1,0:T(8,128)} %right.21, f32[256,128,128]{2,1,0:T(8,128)} %child.21, f32[32,128,128]{2,1,0:T(8,128)} %shard_map.62.after), custom_call_target="tpu_custom_call" | custom-call | flops 3221225472 | bytes 12845056 | tf_op jit(solution)/shard_map/pallas_call | solution.py:65
  68.9 9.1 %shard_map.64.after = f32[32,128,128]{2,1,0:T(8,128)} custom-call(s32[2,32]{1,0:T(2,128)} %labels.45, s32[1]{0:T(128)} %bitcast.me, f32[1024,512]{1,0:T(8,128)} %left.21, f32[512,4096]{1,0:T(8,128)} %right.21, f32[256,128,128]{2,1,0:T(8,128)} %child.21, f32[32,128,128]{2,1,0:T(8,128)} %shard_map.63.after), custom_call_target="tpu_custom_call" | custom-call | flops 3221225472 | bytes 12845056 | tf_op jit(solution)/shard_map/pallas_call | solution.py:65
  78.0 0.0 collective-permute-start.5
  78.0 1.2 collective-permute-start.6
  79.2 0.7 collective-permute-start.9
  79.9 0.0 collective-permute-start.8
  79.9 95.3 %collective-permute-done.8.tiles = f32[4,128,128]{2,1,0:T(8,128)S(1)} collective-permute-done((f32[4,128,128]{2,1,0:T(8,128)}, f32[4,128,128]{2,1,0:T(8,128)S(1)}, u32[]{:S(2)}, u32[]{:S(2)}) %collective-permute-start.8) | collective-permute-done | bytes 262176 | tf_op jit(solution)/shard_map/ppermute | solution.py:260
  175.2 1.6 collective-permute-start.4
  176.8 0.0 collective-permute-done.7.tiles
  176.8 0.0 copy-done
  176.8 0.0 collective-permute-start.3
  176.8 0.0 collective-permute-done.5.tiles
  176.8 0.0 copy-done.1
  176.8 0.0 copy-start.2
  176.8 3.7 collective-permute-start.2
  180.5 0.0 collective-permute-done.6.tiles
  180.5 1.3 copy-done.3
  181.8 1.3 collective-permute-start.1
  183.1 0.0 copy-done.5
  183.1 0.0 collective-permute-done.9.tiles
  183.1 1.4 collective-permute-start
  184.5 9.1 %shard_map.65.tiles = f32[32,128,128]{2,1,0:T(8,128)} custom-call(s32[2,32]{1,0:T(2,128)} %labels.45, s32[1]{0:T(128)} %bitcast.me, f32[1024,512]{1,0:T(8,128)} %left.21, f32[512,4096]{1,0:T(8,128)} %right.21, f32[256,128,128]{2,1,0:T(8,128)} %child.21, f32[32,128,128]{2,1,0:T(8,128)} %shard_map.64.after), custom_call_target="tpu_custom_call" | custom-call | flops 3221225472 | bytes 12845056 | tf_op jit(solution)/shard_map/pallas_call | solution.py:65
  193.6 16.0 %start_front.1.front_in = f32[288,128,128]{2,1,0:T(8,128)} custom-call(s32[2,32]{1,0:T(2,128)} %labels.45, s32[1]{0:T(128)} %bitcast.me, f32[288,128,128]{2,1,0:T(8,128)} %own.1, f32[32,128,128]{2,1,0:T(8,128)} %shard_map.65.tiles), custom_call_target="tpu_custom_call" | custom-call | tf_op jit(solution)/shard_map/start_front/pallas_call | solution.py:101
  209.7 5.1 %shard_map.66.front_in = f32[288,128,128]{2,1,0:T(8,128)} custom-call(s32[2,32]{1,0:T(2,128)} %labels.45, s32[1]{0:T(128)} %bitcast.me, f32[32,128,128]{2,1,0:T(8,128)} %collective-permute-done.9.tiles, f32[288,128,128]{2,1,0:T(8,128)} %start_front.1.front_in), custom_call_target="tpu_custom_call", output_to_operand_aliasing={{}: (3, {})} | custom-call | tf_op jit(solution)/shard_map/pallas_call | solution.py:158
  214.8 3.3 shard_map.67.front_in
  218.0 4.8 %shard_map.68.front_in = f32[288,128,128]{2,1,0:T(8,128)} custom-call(s32[2,32]{1,0:T(2,128)} %labels.45, s32[1]{0:T(128)} %bitcast.me, f32[28,128,128]{2,1,0:T(8,128)} %collective-permute-done.7.tiles, f32[288,128,128]{2,1,0:T(8,128)} %shard_map.67.front_in), custom_call_target="tpu_custom_call", output_to_operand_aliasing={{}: (3, {})} | custom-call | tf_op jit(solution)/shard_map/pallas_call | solution.py:158
  222.9 5.1 %shard_map.69.front_in = f32[288,128,128]{2,1,0:T(8,128)} custom-call(s32[2,32]{1,0:T(2,128)} %labels.45, s32[1]{0:T(128)} %bitcast.me, f32[32,128,128]{2,1,0:T(8,128)} %copy-done.3, f32[288,128,128]{2,1,0:T(8,128)} %shard_map.68.front_in), custom_call_target="tpu_custom_call", output_to_operand_aliasing={{}: (3, {})} | custom-call | tf_op jit(solution)/shard_map/pallas_call | solution.py:158
  227.9 5.1 %shard_map.70.front_in = f32[288,128,128]{2,1,0:T(8,128)} custom-call(s32[2,32]{1,0:T(2,128)} %labels.45, s32[1]{0:T(128)} %bitcast.me, f32[32,128,128]{2,1,0:T(8,128)} %copy-done.2, f32[288,128,128]{2,1,0:T(8,128)} %shard_map.69.front_in), custom_call_target="tpu_custom_call", output_to_operand_aliasing={{}: (3, {})} | custom-call | tf_op jit(solution)/shard_map/pallas_call | solution.py:158
  233.0 0.0 collective-permute-done.4.tiles
  233.0 5.1 %shard_map.71.front_in = f32[288,128,128]{2,1,0:T(8,128)} custom-call(s32[2,32]{1,0:T(2,128)} %labels.45, s32[1]{0:T(128)} %bitcast.me, f32[32,128,128]{2,1,0:T(8,128)} %collective-permute-done.4.tiles, f32[288,128,128]{2,1,0:T(8,128)} %shard_map.70.front_in), custom_call_target="tpu_custom_call", output_to_operand_aliasing={{}: (3, {})} | custom-call | tf_op jit(solution)/shard_map/pallas_call | solution.py:158
  238.1 121.9 %collective-permute-done.3.tiles = f32[32,128,128]{2,1,0:T(8,128)} collective-permute-done((f32[32,128,128]{2,1,0:T(8,128)S(1)}, f32[32,128,128]{2,1,0:T(8,128)}, u32[]{:S(2)}, u32[]{:S(2)}) %collective-permute-start.3) | collective-permute-done | bytes 2097184 | tf_op jit(solution)/shard_map/ppermute | solution.py:260
  360.0 5.1 %shard_map.72.front_in = f32[288,128,128]{2,1,0:T(8,128)} custom-call(s32[2,32]{1,0:T(2,128)} %labels.45, s32[1]{0:T(128)} %bitcast.me, f32[32,128,128]{2,1,0:T(8,128)} %collective-permute-done.3.tiles, f32[288,128,128]{2,1,0:T(8,128)} %shard_map.71.front_in), custom_call_target="tpu_custom_call", output_to_operand_aliasing={{}: (3, {})} | custom-call | tf_op jit(solution)/shard_map/pallas_call | solution.py:158
  365.1 17.5 %collective-permute-done.2.tiles = f32[16,128,128]{2,1,0:T(8,128)} collective-permute-done((f32[16,128,128]{2,1,0:T(8,128)S(1)}, f32[16,128,128]{2,1,0:T(8,128)}, u32[]{:S(2)}, u32[]{:S(2)}) %collective-permute-start.2) | collective-permute-done | bytes 1048608 | tf_op jit(solution)/shard_map/ppermute | solution.py:260
  382.6 4.1 shard_map.73.front_in
  386.6 12.8 %collective-permute-done.1.tiles = f32[12,128,128]{2,1,0:T(8,128)} collective-permute-done((f32[12,128,128]{2,1,0:T(8,128)}, f32[12,128,128]{2,1,0:T(8,128)}, u32[]{:S(2)}, u32[]{:S(2)}) %collective-permute-start.1) | collective-permute-done | bytes 786464 | tf_op jit(solution)/shard_map/ppermute | solution.py:260
  399.4 3.8 shard_map.74.front.front_in
  403.2 2.4 shard_map.75.old
  405.7 0.0 collective-permute-done.tiles
  405.7 2.5 shard_map.76
  (7 shorter events, 0.0 us)
Async XLA Ops:
  13.3 163.4 %collective-permute-start.7 = (f32[28,128,128]{2,1,0:T(8,128)}, f32[28,128,128]{2,1,0:T(8,128)}, u32[]{:S(2)}, u32[]{:S(2)}) collective-permute-start(f32[28,128,128]{2,1,0:T(8,128)} %shard_map.56.after), channel_id=1, source_target_pairs={{0,6},{1,7},{2,4},{3,5},{4,2},{5,3},{6,0},{7,1},{8,14},{9,15},{10,... | collective-permute-start | bytes 5505032 | tf_op jit(solution)/shard_map/ppermute | solution.py:260
  68.9 107.9 %copy-start = (f32[32,128,128]{2,1,0:T(8,128)S(1)}, f32[32,128,128]{2,1,0:T(8,128)}, u32[]{:S(2)}) copy-start(f32[32,128,128]{2,1,0:T(8,128)} %shard_map.57.after) | copy-start | bytes 6291460
  68.9 107.9 %copy-start.1 = (f32[16,128,128]{2,1,0:T(8,128)S(1)}, f32[16,128,128]{2,1,0:T(8,128)}, u32[]{:S(2)}) copy-start(f32[16,128,128]{2,1,0:T(8,128)} %shard_map.59.after) | copy-start | bytes 3145732
  68.9 114.2 %copy-start.4 = (f32[4,128,128]{2,1,0:T(8,128)S(1)}, f32[4,128,128]{2,1,0:T(8,128)}, u32[]{:S(2)}) copy-start(f32[4,128,128]{2,1,0:T(8,128)} %shard_map.61.after) | copy-start | bytes 786436
  78.0 98.8 %collective-permute-start.5 = (f32[32,128,128]{2,1,0:T(8,128)}, f32[32,128,128]{2,1,0:T(8,128)S(1)}, u32[]{:S(2)}, u32[]{:S(2)}) collective-permute-start(f32[32,128,128]{2,1,0:T(8,128)} %shard_map.64.after), channel_id=1, source_target_pairs={{0,3},{1,2},{2,1},{3,0},{4,7},{5,6},{6,5},{7,4},{8,11},{9,10},{10,... | collective-permute-start | bytes 6291464 | tf_op jit(solution)/shard_map/ppermute | solution.py:260
  78.0 102.5 %collective-permute-start.6 = (f32[32,128,128]{2,1,0:T(8,128)}, f32[32,128,128]{2,1,0:T(8,128)S(1)}, u32[]{:S(2)}, u32[]{:S(2)}) collective-permute-start(f32[32,128,128]{2,1,0:T(8,128)} %shard_map.63.after), channel_id=1, source_target_pairs={{0,2},{1,3},{2,0},{3,1},{4,6},{5,7},{6,4},{7,5},{8,10},{9,11},{10,... | collective-permute-start | bytes 6291464 | tf_op jit(solution)/shard_map/ppermute | solution.py:260
  79.2 103.9 %collective-permute-start.9 = (f32[32,128,128]{2,1,0:T(8,128)}, f32[32,128,128]{2,1,0:T(8,128)}, u32[]{:S(2)}, u32[]{:S(2)}) collective-permute-start(f32[32,128,128]{2,1,0:T(8,128)} %shard_map.62.after), channel_id=1, source_target_pairs={{0,1},{1,0},{2,3},{3,2},{4,5},{5,4},{6,7},{7,6},{8,9},{9,8},{10,11... | collective-permute-start | bytes 6291464 | tf_op jit(solution)/shard_map/ppermute | solution.py:260
  79.9 95.3 %collective-permute-start.8 = (f32[4,128,128]{2,1,0:T(8,128)}, f32[4,128,128]{2,1,0:T(8,128)S(1)}, u32[]{:S(2)}, u32[]{:S(2)}) collective-permute-start(f32[4,128,128]{2,1,0:T(8,128)} %shard_map.55.after), channel_id=1, source_target_pairs={{0,6},{1,7},{2,4},{3,5},{4,2},{5,3},{6,0},{7,1},{8,14},{9,15},{10,... | collective-permute-start | bytes 786440 | tf_op jit(solution)/shard_map/ppermute | solution.py:260
  175.2 7.9 %copy-start.5 = (f32[4,128,128]{2,1,0:T(8,128)}, f32[4,128,128]{2,1,0:T(8,128)S(1)}, u32[]{:S(2)}) copy-start(f32[4,128,128]{2,1,0:T(8,128)S(1)} %collective-permute-done.8.tiles) | copy-start | bytes 786436
  175.2 57.8 %collective-permute-start.4 = (f32[32,128,128]{2,1,0:T(8,128)}, f32[32,128,128]{2,1,0:T(8,128)}, u32[]{:S(2)}, u32[]{:S(2)}) collective-permute-start(f32[32,128,128]{2,1,0:T(8,128)} %shard_map.58.after), channel_id=1, source_target_pairs={{0,7},{1,6},{2,5},{3,4},{4,3},{5,2},{6,1},{7,0},{8,15},{9,14},{10,... | collective-permute-start | bytes 6291464 | tf_op jit(solution)/shard_map/ppermute | solution.py:260
  176.8 183.2 %collective-permute-start.3 = (f32[32,128,128]{2,1,0:T(8,128)S(1)}, f32[32,128,128]{2,1,0:T(8,128)}, u32[]{:S(2)}, u32[]{:S(2)}) collective-permute-start(f32[32,128,128]{2,1,0:T(8,128)S(1)} %copy-done), channel_id=1, source_target_pairs={{0,4},{1,5},{2,6},{3,7},{4,0},{5,1},{6,2},{7,3},{8,12},{9,13},{10,... | collective-permute-start | bytes 6291464 | tf_op jit(solution)/shard_map/ppermute | solution.py:260
  176.8 3.7 copy-start.2
  176.8 205.7 %collective-permute-start.2 = (f32[16,128,128]{2,1,0:T(8,128)S(1)}, f32[16,128,128]{2,1,0:T(8,128)}, u32[]{:S(2)}, u32[]{:S(2)}) collective-permute-start(f32[16,128,128]{2,1,0:T(8,128)S(1)} %copy-done.1), channel_id=1, source_target_pairs={{0,5},{1,4},{2,7},{3,6},{4,1},{5,0},{6,3},{7,2},{8,13},{9,12},{10,... | collective-permute-start | bytes 3145736 | tf_op jit(solution)/shard_map/ppermute | solution.py:260
  180.5 1.3 copy-start.3
  181.8 217.6 %collective-permute-start.1 = (f32[12,128,128]{2,1,0:T(8,128)}, f32[12,128,128]{2,1,0:T(8,128)}, u32[]{:S(2)}, u32[]{:S(2)}) collective-permute-start(f32[12,128,128]{2,1,0:T(8,128)} %shard_map.60.after), channel_id=1, source_target_pairs={{0,5},{1,4},{2,7},{3,6},{4,1},{5,0},{6,3},{7,2},{8,13},{9,12},{10,... | collective-permute-start | bytes 2359304 | tf_op jit(solution)/shard_map/ppermute | solution.py:260
  183.1 222.6 %collective-permute-start = (f32[4,128,128]{2,1,0:T(8,128)S(1)}, f32[4,128,128]{2,1,0:T(8,128)}, u32[]{:S(2)}, u32[]{:S(2)}) collective-permute-start(f32[4,128,128]{2,1,0:T(8,128)S(1)} %copy-done.4), channel_id=1, source_target_pairs={{0,5},{1,4},{2,7},{3,6},{4,1},{5,0},{6,3},{7,2},{8,13},{9,12},{10,... | collective-permute-start | bytes 786440 | tf_op jit(solution)/shard_map/ppermute | solution.py:260

commit v2 on v1

--- a/solution.py
+++ b/solution.py
@@ -13,6 +13,7 @@
 PT = 48
 CGR = 4
 PR = 8
+MIB = 1024 * 1024
 
 
 def row_for(labels, me, ncd, dest):
@@ -32,7 +33,7 @@
     return row
 
 
-def stripe_kernel(labels, me, left, right, child, after, out):
+def stripe_kernel(labels, me, left, right, child, out):
     product = jnp.dot(
         left[...], right[...], precision=lax.Precision.HIGHEST, preferred_element_type=jnp.float32
     )
@@ -40,7 +41,7 @@
         out[g] = child[g] - product[:, g * TILE_EDGE : (g + 1) * TILE_EDGE]
 
 
-def stripe(labels, me, l_slab, u_slab, child_tiles, after, ncd, step, first, count, group):
+def stripe(labels, me, l_slab, u_slab, child_tiles, ncd, step, first, count, group):
     panel = l_slab.shape[1]
     groups = MT // group
 
@@ -57,7 +58,6 @@
                 (group, TILE_EDGE, TILE_EDGE),
                 lambda j, lab, who: (row(lab, who) * groups + first // group + j, 0, 0),
             ),
-            pl.BlockSpec(memory_space=pl.ANY),
         ],
         out_specs=pl.BlockSpec((group, TILE_EDGE, TILE_EDGE), lambda j, lab, who: (j, 0, 0)),
     )
@@ -71,7 +71,52 @@
             bytes_accessed=4 * (2 * count * tile + TILE_EDGE * panel * (1 + count)),
             transcendentals=0,
         ),
-    )(labels, me, l_slab, u_slab, child_tiles, after)
+    )(labels, me, l_slab, u_slab, child_tiles)
+
+
+def first_kernel(ncd, step, table, left, right, child, out, labels, rows, columns, sems):
+    count = out.shape[0]
+    fetch = pltpu.make_async_copy(table, labels, sems.at[0])
+    fetch.start()
+    fetch_columns = pltpu.make_async_copy(
+        right.at[:, pl.ds(0, count * TILE_EDGE)], columns, sems.at[1]
+    )
+    fetch_columns.start()
+    fetch.wait()
+    me = lax.axis_index("dev")
+    row = row_for(labels, me, ncd, me ^ step)
+    fetch_rows = pltpu.make_async_copy(
+        left.at[pl.ds(row * TILE_EDGE, TILE_EDGE), :], rows, sems.at[2]
+    )
+    fetch_rows.start()
+    fetch_child = pltpu.make_async_copy(child.at[pl.ds(row * MT, count)], out, sems.at[3])
+    fetch_child.start()
+    fetch_columns.wait()
+    fetch_rows.wait()
+    product = jnp.dot(
+        rows[...], columns[...], precision=lax.Precision.HIGHEST, preferred_element_type=jnp.float32
+    )
+    fetch_child.wait()
+    for g in range(count):
+        out[g] = out[g] - product[:, g * TILE_EDGE : (g + 1) * TILE_EDGE]
+
+
+def first_tiles(labels, l_slab, u_slab, child_tiles, ncd, step, count):
+    shape = (count, TILE_EDGE, TILE_EDGE)
+    panel = l_slab.shape[1]
+    return pl.pallas_call(
+        functools.partial(first_kernel, ncd, step),
+        in_specs=[pl.BlockSpec(memory_space=pl.ANY)] * 4,
+        out_specs=pl.BlockSpec(memory_space=pltpu.VMEM),
+        out_shape=jax.ShapeDtypeStruct(shape, jnp.float32),
+        scratch_shapes=[
+            pltpu.SMEM(labels.shape, labels.dtype),
+            pltpu.VMEM((TILE_EDGE, panel), jnp.float32),
+            pltpu.VMEM((panel, count * TILE_EDGE), jnp.float32),
+            pltpu.SemaphoreType.DMA((4,)),
+        ],
+        compiler_params=pltpu.CompilerParams(vmem_limit_bytes=int(62.4 * MIB)),
+    )(labels, l_slab, u_slab, child_tiles)
 
 
 def start_front_kernel(ncd, labels, me, own, tiles, out):
@@ -114,7 +159,7 @@
     lax.fori_loop(0, count, one, 0)
 
 
-def extend_kernel(ncd, step, first, labels, me, tiles, front_in, front, sums, fetched, stored):
+def extend_kernel(ncd, step, first, labels, me, tiles, front_in, after, front, sums, fetched, stored):
     source = me[0] ^ step
     base = parent_row(labels, me[0], ncd, source) * PT
     child = source // ncd
@@ -139,7 +184,7 @@
     each(count, lambda i: store(i).wait())
 
 
-def extend(labels, me, tiles, front, ncd, step, first):
+def extend(labels, me, tiles, front, after, ncd, step, first):
     count = tiles.shape[0]
     grid_spec = pltpu.PrefetchScalarGridSpec(
         num_scalar_prefetch=2,
@@ -147,6 +192,7 @@
         in_specs=[
             pl.BlockSpec(tiles.shape, lambda i, lab, who: (0, 0, 0)),
             pl.BlockSpec(memory_space=pl.ANY),
+            pl.BlockSpec(memory_space=pl.ANY),
         ],
         out_specs=pl.BlockSpec(memory_space=pl.ANY),
         scratch_shapes=[
@@ -160,7 +206,8 @@
         grid_spec=grid_spec,
         out_shape=jax.ShapeDtypeStruct(front.shape, front.dtype),
         input_output_aliases={3: 0},
-    )(labels, me, tiles, front)
+        compiler_params=pltpu.CompilerParams(vmem_limit_bytes=8 * MIB),
+    )(labels, me, tiles, front, after)
 
 
 def take_kernel(ncd, step, first, labels, me, front, out, fetched):
@@ -206,6 +253,7 @@
         functools.partial(take_kernel, ncd, step, first),
         grid_spec=grid_spec,
         out_shape=jax.ShapeDtypeStruct(shape, jnp.float32),
+        compiler_params=pltpu.CompilerParams(vmem_limit_bytes=50 * MIB),
     )(labels, me, front)
 
 
@@ -226,6 +274,7 @@
         grid_spec=grid_spec,
         out_shape=jax.ShapeDtypeStruct(front.shape, front.dtype),
         input_output_aliases={4: 0},
+        compiler_params=pltpu.CompilerParams(vmem_limit_bytes=3 * MIB),
     )(labels, me, tiles, old, front)
 
 
@@ -233,16 +282,16 @@
     (6, 0, 4, 4),
     (6, 4, 28, 4),
     (4, 0, 32, 8),
-    (7, 0, 32, 8),
-    (5, 0, 16, 8),
-    (5, 16, 12, 4),
-    (5, 28, 4, 4),
+    (5, 0, 32, 8),
+    (7, 0, 16, 8),
+    (7, 16, 12, 4),
+    (7, 28, 4, 4),
     (1, 0, 32, 8),
     (2, 0, 32, 8),
     (3, 0, 32, 8),
 )
-ADDS = ((1, 0), (6, 0), (6, 4), (2, 0), (3, 0), (7, 0), (4, 0), (5, 0), (5, 16))
-LAST = (5, 28)
+ADDS = ((1, 0), (6, 0), (6, 4), (2, 0), (3, 0), (4, 0), (5, 0), (7, 0), (7, 16))
+LAST = (7, 28)
 
 
 def body_rows(child_tiles, l_slab, u_slab, parent_own_entries, parent_label):
@@ -250,22 +299,34 @@
     ncd = ndev // 2
     me = lax.axis_index("dev").astype(jnp.int32).reshape(1)
     arrived = {}
-    after = parent_label
     for step, first, count, group in SENDS:
-        tiles = stripe(
-            parent_label, me, l_slab, u_slab, child_tiles, after, ncd, step, first, count, group
-        )
-        after = tiles
+        if not arrived:
+            tiles = first_tiles(parent_label, l_slab, u_slab, child_tiles, ncd, step, count)
+        else:
+            tiles = stripe(
+                parent_label,
+                me,
+                l_slab,
+                u_slab,
+                child_tiles,
+                ncd,
+                step,
+                first,
+                count,
+                group,
+            )
         pairs = [(d, d ^ step) for d in range(ndev)]
         arrived[step, first] = lax.ppermute(tiles, "dev", pairs)
-    kept = stripe(parent_label, me, l_slab, u_slab, child_tiles, after, ncd, 0, 0, MT, 8)
+    kept = stripe(parent_label, me, l_slab, u_slab, child_tiles, ncd, 0, 0, MT, 8)
     front = start_front(parent_label, me, parent_own_entries, kept, ncd)
-    for step, first in ADDS:
-        front = extend(parent_label, me, arrived[step, first], front, ncd, step, first)
-    step, first = LAST
-    tiles = arrived[step, first]
-    old = take(parent_label, me, front, ncd, step, first, tiles.shape[0])
-    return put(parent_label, me, tiles, old, front, ncd, step, first)
+    for step, first in ADDS[:-1]:
+        tiles = arrived[step, first]
+        front = extend(parent_label, me, tiles, front, parent_label, ncd, step, first)
+    tiles = arrived[LAST]
+    old = take(parent_label, me, front, ncd, *LAST, tiles.shape[0])
+    step, first = ADDS[-1]
+    front = extend(parent_label, me, arrived[step, first], front, old, ncd, step, first)
+    return put(parent_label, me, tiles, old, front, ncd, *LAST)
 
 
 def tile_targets(labels, count, ndev, me_index):

time: 411 us -> 377 us (0.917)
  the two profiles are of different devices: /device:TPU:0 before, /device:TPU:9 now
where the time goes in v2:
time: 377 us; the launch traced here: 375 us
  waiting for transfers between devices  190 us (50%)
  Pallas kernels  137 us (36%)
  starting transfers between devices  47.7 us (13%)
    ppermute x10, waiting for transfers between devices, body_rows(): arrived[step, first] = lax.ppermute(tiles, 'dev', pairs)  190 us
    pallas_call x10, Pallas kernels, stripe(): pl.pallas_call(stripe_kernel, grid_spec=grid_spec, out_shape=jax.ShapeDty...  78.5 us
    ppermute x10, starting transfers between devices, body_rows(): arrived[step, first] = lax.ppermute(tiles, 'dev', pairs)  47.7 us
    pallas_call x9, Pallas kernels, extend(): pl.pallas_call(functools.partial(extend_kernel, ncd, step, first), grid_s...  36.6 us
    pallas_call x1, Pallas kernels, start_front(): pl.pallas_call(functools.partial(start_front_kernel, ncd), grid_spec=grid...  16.1 us
  transfers between devices with their start and end apart: 10, of which 5 were waited for; matrix products, arithmetic and copies ran while one was open for 0% of the time, Pallas kernels for 34%

profile of v2, /device:TPU:9, one launch (start us, length us, event | category | flops | bytes accessed | tf_op | source)
XLA Modules:
  0.0 375.3 jit_solution(2058257818432007661)
XLA Ops:
  0.0 9.9 %shard_map.61 = f32[28,128,128]{2,1,0:T(8,128)} custom-call(s32[2,32]{1,0:T(2,128)} %labels.43, s32[1]{0:T(128)} %bitcast.me, f32[1024,512]{1,0:T(8,128)} %left.21, f32[512,4096]{1,0:T(8,128)} %right.21, f32[256,128,128]{2,1,0:T(8,128)} %child.21), custom_call_target="tpu_custom_call" | custom-call | flops 2818572288 | bytes 11272192 | tf_op jit(solution)/shard_map/pallas_call | solution.py:65
  9.9 1.3 collective-permute-start.6
  11.2 8.9 %shard_map.63 = f32[32,128,128]{2,1,0:T(8,128)} custom-call(s32[2,32]{1,0:T(2,128)} %labels.43, s32[1]{0:T(128)} %bitcast.me, f32[1024,512]{1,0:T(8,128)} %left.21, f32[512,4096]{1,0:T(8,128)} %right.21, f32[256,128,128]{2,1,0:T(8,128)} %child.21), custom_call_target="tpu_custom_call" | custom-call | flops 3221225472 | bytes 12845056 | tf_op jit(solution)/shard_map/pallas_call | solution.py:65
  20.1 1.0 collective-permute-start.8
  21.1 3.2 shard_map.62
  24.3 0.2 collective-permute-start.7
  24.5 8.9 %shard_map.60 = f32[32,128,128]{2,1,0:T(8,128)} custom-call(s32[2,32]{1,0:T(2,128)} %labels.43, s32[1]{0:T(128)} %bitcast.me, f32[1024,512]{1,0:T(8,128)} %left.21, f32[512,4096]{1,0:T(8,128)} %right.21, f32[256,128,128]{2,1,0:T(8,128)} %child.21), custom_call_target="tpu_custom_call" | custom-call | flops 3221225472 | bytes 12845056 | tf_op jit(solution)/shard_map/pallas_call | solution.py:65
  33.4 2.0 collective-permute-start.5
  35.5 8.9 %shard_map.59 = f32[32,128,128]{2,1,0:T(8,128)} custom-call(s32[2,32]{1,0:T(2,128)} %labels.43, s32[1]{0:T(128)} %bitcast.me, f32[1024,512]{1,0:T(8,128)} %left.21, f32[512,4096]{1,0:T(8,128)} %right.21, f32[256,128,128]{2,1,0:T(8,128)} %child.21), custom_call_target="tpu_custom_call" | custom-call | flops 3221225472 | bytes 12845056 | tf_op jit(solution)/shard_map/pallas_call | solution.py:65
  44.4 0.0 collective-permute-start.4
  44.4 8.9 %shard_map.58 = f32[32,128,128]{2,1,0:T(8,128)} custom-call(s32[2,32]{1,0:T(2,128)} %labels.43, s32[1]{0:T(128)} %bitcast.me, f32[1024,512]{1,0:T(8,128)} %left.21, f32[512,4096]{1,0:T(8,128)} %right.21, f32[256,128,128]{2,1,0:T(8,128)} %child.21), custom_call_target="tpu_custom_call" | custom-call | flops 3221225472 | bytes 12845056 | tf_op jit(solution)/shard_map/pallas_call | solution.py:65
  53.3 8.9 %shard_map.57 = f32[32,128,128]{2,1,0:T(8,128)} custom-call(s32[2,32]{1,0:T(2,128)} %labels.43, s32[1]{0:T(128)} %bitcast.me, f32[1024,512]{1,0:T(8,128)} %left.21, f32[512,4096]{1,0:T(8,128)} %right.21, f32[256,128,128]{2,1,0:T(8,128)} %child.21), custom_call_target="tpu_custom_call" | custom-call | flops 3221225472 | bytes 12845056 | tf_op jit(solution)/shard_map/pallas_call | solution.py:65
  62.2 39.6 %collective-permute-done.7.tiles = f32[4,128,128]{2,1,0:T(8,128)S(1)} collective-permute-done((f32[4,128,128]{2,1,0:T(8,128)}, f32[4,128,128]{2,1,0:T(8,128)S(1)}, u32[]{:S(2)}, u32[]{:S(2)}) %collective-permute-start.7) | collective-permute-done | bytes 262176 | tf_op jit(solution)/shard_map/ppermute | solution.py:319
  101.8 0.0 copy-start.1
  101.8 0.0 collective-permute-start.3
  101.8 0.0 collective-permute-done.6.tiles
  101.8 3.9 %collective-permute-start.2 = (f32[32,128,128]{2,1,0:T(8,128)}, f32[32,128,128]{2,1,0:T(8,128)}, u32[]{:S(2)}, u32[]{:S(2)}) collective-permute-start(f32[32,128,128]{2,1,0:T(8,128)} %shard_map.57), channel_id=1, source_target_pairs={{0,5},{1,4},{2,7},{3,6},{4,1},{5,0},{6,3},{7,2},{8,13},{9,12},{10,... | collective-permute-start | bytes 6291464 | tf_op jit(solution)/shard_map/ppermute | solution.py:319
  105.7 5.8 %shard_map.56 = f32[16,128,128]{2,1,0:T(8,128)} custom-call(s32[2,32]{1,0:T(2,128)} %labels.43, s32[1]{0:T(128)} %bitcast.me, f32[1024,512]{1,0:T(8,128)} %left.21, f32[512,4096]{1,0:T(8,128)} %right.21, f32[256,128,128]{2,1,0:T(8,128)} %child.21), custom_call_target="tpu_custom_call" | custom-call | flops 1610612736 | bytes 6553600 | tf_op jit(solution)/shard_map/pallas_call | solution.py:65
  111.4 0.0 copy-done.1
  111.4 0.0 collective-permute-done.8.tiles
  111.4 0.1 collective-permute-start.1
  111.5 5.7 %shard_map.74 = f32[12,128,128]{2,1,0:T(8,128)} custom-call(s32[2,32]{1,0:T(2,128)} %labels.43, s32[1]{0:T(128)} %bitcast.me, f32[1024,512]{1,0:T(8,128)} %left.21, f32[512,4096]{1,0:T(8,128)} %right.21, f32[256,128,128]{2,1,0:T(8,128)} %child.21), custom_call_target="tpu_custom_call" | custom-call | flops 1207959552 | bytes 4980736 | tf_op jit(solution)/shard_map/pallas_call | solution.py:65
  117.2 0.0 collective-permute-done.5.tiles
  117.2 34.5 %collective-permute-start.9 = (f32[12,128,128]{2,1,0:T(8,128)}, f32[12,128,128]{2,1,0:T(8,128)}, u32[]{:S(2)}, u32[]{:S(2)}) collective-permute-start(f32[12,128,128]{2,1,0:T(8,128)} %shard_map.74), channel_id=1, source_target_pairs={{0,7},{1,6},{2,5},{3,4},{4,3},{5,2},{6,1},{7,0},{8,15},{9,14},{10,... | collective-permute-start | bytes 2359304 | tf_op jit(solution)/shard_map/ppermute | solution.py:319
  151.7 3.4 shard_map.55
  155.1 36.8 %collective-permute-done.4.tiles = f32[32,128,128]{2,1,0:T(8,128)} collective-permute-done((f32[32,128,128]{2,1,0:T(8,128)}, f32[32,128,128]{2,1,0:T(8,128)}, u32[]{:S(2)}, u32[]{:S(2)}) %collective-permute-start.4) | collective-permute-done | bytes 2097184 | tf_op jit(solution)/shard_map/ppermute | solution.py:319
  192.0 4.7 %collective-permute-start = (f32[4,128,128]{2,1,0:T(8,128)}, f32[4,128,128]{2,1,0:T(8,128)S(1)}, u32[]{:S(2)}, u32[]{:S(2)}) collective-permute-start(f32[4,128,128]{2,1,0:T(8,128)} %shard_map.55), channel_id=1, source_target_pairs={{0,7},{1,6},{2,5},{3,4},{4,3},{5,2},{6,1},{7,0},{8,15},{9,14},{10,... | collective-permute-start | bytes 786440 | tf_op jit(solution)/shard_map/ppermute | solution.py:319
  196.6 9.1 %shard_map.64.tiles = f32[32,128,128]{2,1,0:T(8,128)} custom-call(s32[2,32]{1,0:T(2,128)} %labels.43, s32[1]{0:T(128)} %bitcast.me, f32[1024,512]{1,0:T(8,128)} %left.21, f32[512,4096]{1,0:T(8,128)} %right.21, f32[256,128,128]{2,1,0:T(8,128)} %child.21), custom_call_target="tpu_custom_call" | custom-call | flops 3221225472 | bytes 12845056 | tf_op jit(solution)/shard_map/pallas_call | solution.py:65
  205.8 0.0 copy-start
  205.8 16.1 %start_front.1.front_in = f32[288,128,128]{2,1,0:T(8,128)} custom-call(s32[2,32]{1,0:T(2,128)} %labels.43, s32[1]{0:T(128)} %bitcast.me, f32[288,128,128]{2,1,0:T(8,128)} %own.1, f32[32,128,128]{2,1,0:T(8,128)} %shard_map.64.tiles), custom_call_target="tpu_custom_call" | custom-call | tf_op jit(solution)/shard_map/start_front/pallas_call | solution.py:146
  221.8 0.0 copy-done
  221.8 4.9 %shard_map.65.front_in = f32[288,128,128]{2,1,0:T(8,128)} custom-call(s32[2,32]{1,0:T(2,128)S(1)} %copy-done, s32[1]{0:T(128)} %bitcast.me, f32[32,128,128]{2,1,0:T(8,128)} %collective-permute-done.8.tiles, f32[288,128,128]{2,1,0:T(8,128)} %start_front.1.front_in, s32[2,32]{1,0:T(2,128)S(1)} %copy-done), custom_call_target="tpu_custom_call", output_to_operand_aliasing={{}: (3, {})} | custom-call | tf_op jit(solution)/shard_map/pallas_call | solution.py:204
  226.8 0.0 copy-done.2
  226.8 2.3 shard_map.66.front_in
  229.1 4.7 %shard_map.67.front_in = f32[288,128,128]{2,1,0:T(8,128)} custom-call(s32[2,32]{1,0:T(2,128)S(1)} %copy-done, s32[1]{0:T(128)} %bitcast.me, f32[28,128,128]{2,1,0:T(8,128)} %collective-permute-done.6.tiles, f32[288,128,128]{2,1,0:T(8,128)} %shard_map.66.front_in, s32[2,32]{1,0:T(2,128)S(1)} %copy-done), custom_call_target="tpu_custom_call", output_to_operand_aliasing={{}: (3, {})} | custom-call | tf_op jit(solution)/shard_map/pallas_call | solution.py:204
  233.7 3.4 shard_map.68.front_in
  237.2 4.9 %shard_map.69.front_in = f32[288,128,128]{2,1,0:T(8,128)} custom-call(s32[2,32]{1,0:T(2,128)S(1)} %copy-done, s32[1]{0:T(128)} %bitcast.me, f32[32,128,128]{2,1,0:T(8,128)} %collective-permute-done.4.tiles, f32[288,128,128]{2,1,0:T(8,128)} %shard_map.68.front_in, s32[2,32]{1,0:T(2,128)S(1)} %copy-done), custom_call_target="tpu_custom_call", output_to_operand_aliasing={{}: (3, {})} | custom-call | tf_op jit(solution)/shard_map/pallas_call | solution.py:204
  242.1 0.0 collective-permute-done.3.tiles
  242.1 4.9 %shard_map.70.front_in = f32[288,128,128]{2,1,0:T(8,128)} custom-call(s32[2,32]{1,0:T(2,128)S(1)} %copy-done, s32[1]{0:T(128)} %bitcast.me, f32[32,128,128]{2,1,0:T(8,128)} %collective-permute-done.3.tiles, f32[288,128,128]{2,1,0:T(8,128)} %shard_map.69.front_in, s32[2,32]{1,0:T(2,128)S(1)} %copy-done), custom_call_target="tpu_custom_call", output_to_operand_aliasing={{}: (3, {})} | custom-call | tf_op jit(solution)/shard_map/pallas_call | solution.py:204
  247.1 78.8 %collective-permute-done.2.tiles = f32[32,128,128]{2,1,0:T(8,128)} collective-permute-done((f32[32,128,128]{2,1,0:T(8,128)}, f32[32,128,128]{2,1,0:T(8,128)}, u32[]{:S(2)}, u32[]{:S(2)}) %collective-permute-start.2) | collective-permute-done | bytes 2097184 | tf_op jit(solution)/shard_map/ppermute | solution.py:319
  325.9 4.9 %shard_map.71.front_in = f32[288,128,128]{2,1,0:T(8,128)} custom-call(s32[2,32]{1,0:T(2,128)S(1)} %copy-done, s32[1]{0:T(128)} %bitcast.me, f32[32,128,128]{2,1,0:T(8,128)} %collective-permute-done.2.tiles, f32[288,128,128]{2,1,0:T(8,128)} %shard_map.70.front_in, s32[2,32]{1,0:T(2,128)S(1)} %copy-done), custom_call_target="tpu_custom_call", output_to_operand_aliasing={{}: (3, {})} | custom-call | tf_op jit(solution)/shard_map/pallas_call | solution.py:204
  330.8 22.5 %collective-permute-done.1.tiles = f32[16,128,128]{2,1,0:T(8,128)S(1)} collective-permute-done((f32[16,128,128]{2,1,0:T(8,128)}, f32[16,128,128]{2,1,0:T(8,128)S(1)}, u32[]{:S(2)}, u32[]{:S(2)}) %collective-permute-start.1) | collective-permute-done | bytes 1048608 | tf_op jit(solution)/shard_map/ppermute | solution.py:319
  353.3 2.8 shard_map.72.front.front_in
  356.1 1.6 shard_map.73.after.old
  357.8 12.3 %collective-permute-done.9.tiles = f32[12,128,128]{2,1,0:T(8,128)} collective-permute-done((f32[12,128,128]{2,1,0:T(8,128)}, f32[12,128,128]{2,1,0:T(8,128)}, u32[]{:S(2)}, u32[]{:S(2)}) %collective-permute-start.9) | collective-permute-done | bytes 786464 | tf_op jit(solution)/shard_map/ppermute | solution.py:319
  370.1 3.7 shard_map.75.front_in
  373.8 0.0 collective-permute-done.tiles
  373.8 1.4 shard_map.76
  (1 shorter events, 0.0 us)
Async XLA Ops:
  9.9 91.9 %collective-permute-start.6 = (f32[28,128,128]{2,1,0:T(8,128)}, f32[28,128,128]{2,1,0:T(8,128)}, u32[]{:S(2)}, u32[]{:S(2)}) collective-permute-start(f32[28,128,128]{2,1,0:T(8,128)} %shard_map.61), channel_id=1, source_target_pairs={{0,6},{1,7},{2,4},{3,5},{4,2},{5,3},{6,0},{7,1},{8,14},{9,15},{10,... | collective-permute-start | bytes 5505032 | tf_op jit(solution)/shard_map/ppermute | solution.py:319
  20.1 91.3 %collective-permute-start.8 = (f32[32,128,128]{2,1,0:T(8,128)}, f32[32,128,128]{2,1,0:T(8,128)}, u32[]{:S(2)}, u32[]{:S(2)}) collective-permute-start(f32[32,128,128]{2,1,0:T(8,128)} %shard_map.63), channel_id=1, source_target_pairs={{0,1},{1,0},{2,3},{3,2},{4,5},{5,4},{6,7},{7,6},{8,9},{9,8},{10,11... | collective-permute-start | bytes 6291464 | tf_op jit(solution)/shard_map/ppermute | solution.py:319
  24.3 77.5 %collective-permute-start.7 = (f32[4,128,128]{2,1,0:T(8,128)}, f32[4,128,128]{2,1,0:T(8,128)S(1)}, u32[]{:S(2)}, u32[]{:S(2)}) collective-permute-start(f32[4,128,128]{2,1,0:T(8,128)} %shard_map.62), channel_id=1, source_target_pairs={{0,6},{1,7},{2,4},{3,5},{4,2},{5,3},{6,0},{7,1},{8,14},{9,15},{10,... | collective-permute-start | bytes 786440 | tf_op jit(solution)/shard_map/ppermute | solution.py:319
  33.4 83.8 %collective-permute-start.5 = (f32[32,128,128]{2,1,0:T(8,128)}, f32[32,128,128]{2,1,0:T(8,128)S(1)}, u32[]{:S(2)}, u32[]{:S(2)}) collective-permute-start(f32[32,128,128]{2,1,0:T(8,128)} %shard_map.60), channel_id=1, source_target_pairs={{0,2},{1,3},{2,0},{3,1},{4,6},{5,7},{6,4},{7,5},{8,10},{9,11},{10,... | collective-permute-start | bytes 6291464 | tf_op jit(solution)/shard_map/ppermute | solution.py:319
  44.4 147.6 %collective-permute-start.4 = (f32[32,128,128]{2,1,0:T(8,128)}, f32[32,128,128]{2,1,0:T(8,128)}, u32[]{:S(2)}, u32[]{:S(2)}) collective-permute-start(f32[32,128,128]{2,1,0:T(8,128)} %shard_map.59), channel_id=1, source_target_pairs={{0,3},{1,2},{2,1},{3,0},{4,7},{5,6},{6,5},{7,4},{8,11},{9,10},{10,... | collective-permute-start | bytes 6291464 | tf_op jit(solution)/shard_map/ppermute | solution.py:319
  101.8 9.7 %copy-start.1 = (f32[4,128,128]{2,1,0:T(8,128)}, f32[4,128,128]{2,1,0:T(8,128)S(1)}, u32[]{:S(2)}) copy-start(f32[4,128,128]{2,1,0:T(8,128)S(1)} %collective-permute-done.7.tiles) | copy-start | bytes 786436
  101.8 140.3 %collective-permute-start.3 = (f32[32,128,128]{2,1,0:T(8,128)}, f32[32,128,128]{2,1,0:T(8,128)}, u32[]{:S(2)}, u32[]{:S(2)}) collective-permute-start(f32[32,128,128]{2,1,0:T(8,128)} %shard_map.58), channel_id=1, source_target_pairs={{0,4},{1,5},{2,6},{3,7},{4,0},{5,1},{6,2},{7,3},{8,12},{9,13},{10,... | collective-permute-start | bytes 6291464 | tf_op jit(solution)/shard_map/ppermute | solution.py:319
  101.8 224.1 %collective-permute-start.2 = (f32[32,128,128]{2,1,0:T(8,128)}, f32[32,128,128]{2,1,0:T(8,128)}, u32[]{:S(2)}, u32[]{:S(2)}) collective-permute-start(f32[32,128,128]{2,1,0:T(8,128)} %shard_map.57), channel_id=1, source_target_pairs={{0,5},{1,4},{2,7},{3,6},{4,1},{5,0},{6,3},{7,2},{8,13},{9,12},{10,... | collective-permute-start | bytes 6291464 | tf_op jit(solution)/shard_map/ppermute | solution.py:319
  111.4 241.9 %collective-permute-start.1 = (f32[16,128,128]{2,1,0:T(8,128)}, f32[16,128,128]{2,1,0:T(8,128)S(1)}, u32[]{:S(2)}, u32[]{:S(2)}) collective-permute-start(f32[16,128,128]{2,1,0:T(8,128)} %shard_map.56), channel_id=1, source_target_pairs={{0,7},{1,6},{2,5},{3,4},{4,3},{5,2},{6,1},{7,0},{8,15},{9,14},{10,... | collective-permute-start | bytes 3145736 | tf_op jit(solution)/shard_map/ppermute | solution.py:319
  117.2 252.9 %collective-permute-start.9 = (f32[12,128,128]{2,1,0:T(8,128)}, f32[12,128,128]{2,1,0:T(8,128)}, u32[]{:S(2)}, u32[]{:S(2)}) collective-permute-start(f32[12,128,128]{2,1,0:T(8,128)} %shard_map.74), channel_id=1, source_target_pairs={{0,7},{1,6},{2,5},{3,4},{4,3},{5,2},{6,1},{7,0},{8,15},{9,14},{10,... | collective-permute-start | bytes 2359304 | tf_op jit(solution)/shard_map/ppermute | solution.py:319
  192.0 181.8 %collective-permute-start = (f32[4,128,128]{2,1,0:T(8,128)}, f32[4,128,128]{2,1,0:T(8,128)S(1)}, u32[]{:S(2)}, u32[]{:S(2)}) collective-permute-start(f32[4,128,128]{2,1,0:T(8,128)} %shard_map.55), channel_id=1, source_target_pairs={{0,7},{1,6},{2,5},{3,4},{4,3},{5,2},{6,1},{7,0},{8,15},{9,14},{10,... | collective-permute-start | bytes 786440 | tf_op jit(solution)/shard_map/ppermute | solution.py:319
  205.8 16.1 %copy-start = (s32[2,32]{1,0:T(2,128)S(1)}, s32[2,32]{1,0:T(2,128)}, u32[]{:S(2)}) copy-start(s32[2,32]{1,0:T(2,128)} %labels.43) | copy-start | bytes 772
  221.8 4.9 %copy-start.2 = (f32[4,128,128]{2,1,0:T(8,128)S(1)}, f32[4,128,128]{2,1,0:T(8,128)}, u32[]{:S(2)}) copy-start(f32[4,128,128]{2,1,0:T(8,128)} %copy-done.1) | copy-start | bytes 786436

commit v3 on v2

--- a/solution.py
+++ b/solution.py
@@ -14,6 +14,7 @@
 CGR = 4
 PR = 8
 MIB = 1024 * 1024
+VMEM_LIMIT = int(62.5 * MIB)
 
 
 def row_for(labels, me, ncd, dest):
@@ -71,6 +72,7 @@
             bytes_accessed=4 * (2 * count * tile + TILE_EDGE * panel * (1 + count)),
             transcendentals=0,
         ),
+        compiler_params=pltpu.CompilerParams(vmem_limit_bytes=VMEM_LIMIT),
     )(labels, me, l_slab, u_slab, child_tiles)
 
 
@@ -104,6 +106,7 @@
 def first_tiles(labels, l_slab, u_slab, child_tiles, ncd, step, count):
     shape = (count, TILE_EDGE, TILE_EDGE)
     panel = l_slab.shape[1]
+    arrays = (labels, l_slab, u_slab, child_tiles)
     return pl.pallas_call(
         functools.partial(first_kernel, ncd, step),
         in_specs=[pl.BlockSpec(memory_space=pl.ANY)] * 4,
@@ -115,8 +118,8 @@
             pltpu.VMEM((panel, count * TILE_EDGE), jnp.float32),
             pltpu.SemaphoreType.DMA((4,)),
         ],
-        compiler_params=pltpu.CompilerParams(vmem_limit_bytes=int(62.4 * MIB)),
-    )(labels, l_slab, u_slab, child_tiles)
+        compiler_params=pltpu.CompilerParams(vmem_limit_bytes=8 * MIB),
+    )(*(pltpu.with_memory_space_constraint(x, pltpu.HBM) for x in arrays))
 
 
 def start_front_kernel(ncd, labels, me, own, tiles, out):
@@ -147,6 +150,7 @@
         functools.partial(start_front_kernel, ncd),
         grid_spec=grid_spec,
         out_shape=jax.ShapeDtypeStruct(own.shape, own.dtype),
+        compiler_params=pltpu.CompilerParams(vmem_limit_bytes=VMEM_LIMIT),
         name="start_front",
     )(labels, me, own, tiles)
 
@@ -159,33 +163,28 @@
     lax.fori_loop(0, count, one, 0)
 
 
-def extend_kernel(ncd, step, first, labels, me, tiles, front_in, after, front, sums, fetched, stored):
-    source = me[0] ^ step
-    base = parent_row(labels, me[0], ncd, source) * PT
+def slots_of(ncd, step, first, labels, me, front):
+    source = me ^ step
+    base = parent_row(labels, me, ncd, source) * PT
     child = source // ncd
+    return lambda i: front.at[base + labels[child, first + i]]
+
+
+def extend_kernel(ncd, step, first, labels, me, tiles, front_in, after, front, sums, sems):
+    slot = slots_of(ncd, step, first, labels, me[0], front)
     count = tiles.shape[0]
-
-    def slot(i):
-        return front.at[base + labels[child, first + i]]
-
-    def fetch(i):
-        return pltpu.make_async_copy(slot(i), sums.at[i], fetched.at[i])
-
-    def store(i):
-        return pltpu.make_async_copy(sums.at[i], slot(i), stored.at[i])
+    each(count, lambda i: pltpu.make_async_copy(slot(i), sums.at[i], sems.at[0]).start())
+    pltpu.make_async_copy(sums, sums, sems.at[0]).wait()
 
     def add(i):
-        fetch(i).wait()
         sums[i] = sums[i] + tiles[i]
-        store(i).start()
-
-    each(count, lambda i: fetch(i).start())
+        pltpu.make_async_copy(sums.at[i], slot(i), sems.at[1]).start()
+
     each(count, add)
-    each(count, lambda i: store(i).wait())
+    pltpu.make_async_copy(sums, sums, sems.at[1]).wait()
 
 
 def extend(labels, me, tiles, front, after, ncd, step, first):
-    count = tiles.shape[0]
     grid_spec = pltpu.PrefetchScalarGridSpec(
         num_scalar_prefetch=2,
         grid=(1,),
@@ -197,8 +196,7 @@
         out_specs=pl.BlockSpec(memory_space=pl.ANY),
         scratch_shapes=[
             pltpu.VMEM(tiles.shape, jnp.float32),
-            pltpu.SemaphoreType.DMA((count,)),
-            pltpu.SemaphoreType.DMA((count,)),
+            pltpu.SemaphoreType.DMA((2,)),
         ],
     )
     return pl.pallas_call(
@@ -210,34 +208,21 @@
     )(labels, me, tiles, front, after)
 
 
-def take_kernel(ncd, step, first, labels, me, front, out, fetched):
-    source = me[0] ^ step
-    base = parent_row(labels, me[0], ncd, source) * PT
-    child = source // ncd
-
-    def fetch(i):
-        slot = base + labels[child, first + i]
-        return pltpu.make_async_copy(front.at[slot], out.at[i], fetched.at[i])
-
-    each(out.shape[0], lambda i: fetch(i).start())
-    each(out.shape[0], lambda i: fetch(i).wait())
-
-
-def put_kernel(ncd, step, first, labels, me, tiles, old, front_in, front, sums, stored):
-    source = me[0] ^ step
-    base = parent_row(labels, me[0], ncd, source) * PT
-    child = source // ncd
-
-    def store(i):
-        slot = base + labels[child, first + i]
-        return pltpu.make_async_copy(sums.at[i], front.at[slot], stored.at[i])
+def take_kernel(ncd, step, first, labels, me, front, out, sem):
+    slot = slots_of(ncd, step, first, labels, me[0], front)
+    each(out.shape[0], lambda i: pltpu.make_async_copy(slot(i), out.at[i], sem.at[0]).start())
+    pltpu.make_async_copy(out, out, sem.at[0]).wait()
+
+
+def put_kernel(ncd, step, first, labels, me, tiles, old, front_in, front, sums, sem):
+    slot = slots_of(ncd, step, first, labels, me[0], front)
 
     def add(i):
         sums[i] = old[i] + tiles[i]
-        store(i).start()
+        pltpu.make_async_copy(sums.at[i], slot(i), sem.at[0]).start()
 
     each(tiles.shape[0], add)
-    each(tiles.shape[0], lambda i: store(i).wait())
+    pltpu.make_async_copy(sums, sums, sem.at[0]).wait()
 
 
 def take(labels, me, front, ncd, step, first, count):
@@ -247,7 +232,7 @@
         grid=(1,),
         in_specs=[pl.BlockSpec(memory_space=pl.ANY)],
         out_specs=pl.BlockSpec(shape, lambda i, lab, who: (0, 0, 0)),
-        scratch_shapes=[pltpu.SemaphoreType.DMA((count,))],
+        scratch_shapes=[pltpu.SemaphoreType.DMA((1,))],
     )
     return pl.pallas_call(
         functools.partial(take_kernel, ncd, step, first),
@@ -258,15 +243,14 @@
 
 
 def put(labels, me, tiles, old, front, ncd, step, first):
-    block = pl.BlockSpec(tiles.shape, lambda i, lab, who: (0, 0, 0))
+    block = pl.BlockSpec(memory_space=pltpu.VMEM)
     grid_spec = pltpu.PrefetchScalarGridSpec(
         num_scalar_prefetch=2,
-        grid=(1,),
         in_specs=[block, block, pl.BlockSpec(memory_space=pl.ANY)],
         out_specs=pl.BlockSpec(memory_space=pl.ANY),
         scratch_shapes=[
             pltpu.VMEM(tiles.shape, jnp.float32),
-            pltpu.SemaphoreType.DMA((tiles.shape[0],)),
+            pltpu.SemaphoreType.DMA((1,)),
         ],
     )
     return pl.pallas_call(
@@ -283,15 +267,14 @@
     (6, 4, 28, 4),
     (4, 0, 32, 8),
     (5, 0, 32, 8),
-    (7, 0, 16, 8),
-    (7, 16, 12, 4),
-    (7, 28, 4, 4),
+    (7, 0, 26, 2),
+    (7, 26, 6, 2),
     (1, 0, 32, 8),
     (2, 0, 32, 8),
     (3, 0, 32, 8),
 )
-ADDS = ((1, 0), (6, 0), (6, 4), (2, 0), (3, 0), (4, 0), (5, 0), (7, 0), (7, 16))
-LAST = (7, 28)
+ADDS = ((1, 0), (6, 0), (6, 4), (2, 0), (3, 0), (4, 0), (5, 0), (7, 0))
+LAST = (7, 26)
 
 
 def body_rows(child_tiles, l_slab, u_slab, parent_own_entries, parent_label):

time: 377 us -> 377 us (level)
  starting transfers between devices: 47.7 us -> 36 us
  waiting for transfers between devices: 190 us -> 199 us
    ppermute x10 -> x9, starting transfers between devices: 47.7 us -> 36 us  [body_rows(): arrived[step, first] = lax.ppermute(tiles, 'dev', pairs)]
    ppermute x10 -> x9, waiting for transfers between devices: 190 us -> 199 us  [body_rows(): arrived[step, first] = lax.ppermute(tiles, 'dev', pairs)]
    pallas_call x10 -> x9, Pallas kernels: 78.5 us -> 81.4 us  [stripe(): pl.pallas_call(stripe_kernel, grid_spec=grid_spec, out_shape=jax.ShapeDty...]
    pallas_call x9 -> x8, Pallas kernels: 36.6 us -> 36.7 us  [extend(): pl.pallas_call(functools.partial(extend_kernel, ncd, step, first), grid_s...]
  transfers between devices with their start and end apart: 10 -> 9, of which waited for: 5 -> 4; matrix products, arithmetic and copies ran while one was open for 0% -> 0% of each run, Pallas kernels for 34% -> 34%
where the time goes in v3:
time: 377 us; the launch traced here: 375 us
  waiting for transfers between devices  199 us (53%)
  Pallas kernels  140 us (37%)
  starting transfers between devices  36 us (10%)
    ppermute x9, waiting for transfers between devices, body_rows(): arrived[step, first] = lax.ppermute(tiles, 'dev', pairs)  199 us
    pallas_call x9, Pallas kernels, stripe(): pl.pallas_call(stripe_kernel, grid_spec=grid_spec, out_shape=jax.ShapeDty...  81.4 us
    pallas_call x8, Pallas kernels, extend(): pl.pallas_call(functools.partial(extend_kernel, ncd, step, first), grid_s...  36.7 us
    ppermute x9, starting transfers between devices, body_rows(): arrived[step, first] = lax.ppermute(tiles, 'dev', pairs)  36 us
    pallas_call x1, Pallas kernels, start_front(): pl.pallas_call(functools.partial(start_front_kernel, ncd), grid_spec=grid...  16.1 us
  transfers between devices with their start and end apart: 9, of which 4 were waited for; matrix products, arithmetic and copies ran while one was open for 0% of the time, Pallas kernels for 34%

profile of v3, /device:TPU:9, one launch (start us, length us, event | category | flops | bytes accessed | tf_op | source)
XLA Modules:
  0.0 375.2 jit_solution(3389744669674653307)
XLA Ops:
  0.0 9.9 %shard_map.60 = f32[28,128,128]{2,1,0:T(8,128)} custom-call(s32[2,32]{1,0:T(2,128)} %labels.39, s32[1]{0:T(128)} %bitcast.me, f32[1024,512]{1,0:T(8,128)} %left.19, f32[512,4096]{1,0:T(8,128)} %right.19, f32[256,128,128]{2,1,0:T(8,128)} %child.19), custom_call_target="tpu_custom_call" | custom-call | flops 2818572288 | bytes 11272192 | tf_op jit(solution)/shard_map/pallas_call | solution.py:66
  9.9 1.3 collective-permute-start.5
  11.2 8.9 %shard_map.62 = f32[32,128,128]{2,1,0:T(8,128)} custom-call(s32[2,32]{1,0:T(2,128)} %labels.39, s32[1]{0:T(128)} %bitcast.me, f32[1024,512]{1,0:T(8,128)} %left.19, f32[512,4096]{1,0:T(8,128)} %right.19, f32[256,128,128]{2,1,0:T(8,128)} %child.19), custom_call_target="tpu_custom_call" | custom-call | flops 3221225472 | bytes 12845056 | tf_op jit(solution)/shard_map/pallas_call | solution.py:66
  20.1 1.0 collective-permute-start.7
  21.0 2.5 shard_map.61
  23.5 0.2 collective-permute-start.6
  23.8 8.9 %shard_map.59 = f32[32,128,128]{2,1,0:T(8,128)} custom-call(s32[2,32]{1,0:T(2,128)} %labels.39, s32[1]{0:T(128)} %bitcast.me, f32[1024,512]{1,0:T(8,128)} %left.19, f32[512,4096]{1,0:T(8,128)} %right.19, f32[256,128,128]{2,1,0:T(8,128)} %child.19), custom_call_target="tpu_custom_call" | custom-call | flops 3221225472 | bytes 12845056 | tf_op jit(solution)/shard_map/pallas_call | solution.py:66
  32.7 2.0 collective-permute-start.4
  34.7 8.9 %shard_map.58 = f32[32,128,128]{2,1,0:T(8,128)} custom-call(s32[2,32]{1,0:T(2,128)} %labels.39, s32[1]{0:T(128)} %bitcast.me, f32[1024,512]{1,0:T(8,128)} %left.19, f32[512,4096]{1,0:T(8,128)} %right.19, f32[256,128,128]{2,1,0:T(8,128)} %child.19), custom_call_target="tpu_custom_call" | custom-call | flops 3221225472 | bytes 12845056 | tf_op jit(solution)/shard_map/pallas_call | solution.py:66
  43.6 0.0 collective-permute-start.3
  43.6 8.9 %shard_map.57 = f32[32,128,128]{2,1,0:T(8,128)} custom-call(s32[2,32]{1,0:T(2,128)} %labels.39, s32[1]{0:T(128)} %bitcast.me, f32[1024,512]{1,0:T(8,128)} %left.19, f32[512,4096]{1,0:T(8,128)} %right.19, f32[256,128,128]{2,1,0:T(8,128)} %child.19), custom_call_target="tpu_custom_call" | custom-call | flops 3221225472 | bytes 12845056 | tf_op jit(solution)/shard_map/pallas_call | solution.py:66
  52.5 8.9 %shard_map.56 = f32[32,128,128]{2,1,0:T(8,128)} custom-call(s32[2,32]{1,0:T(2,128)} %labels.39, s32[1]{0:T(128)} %bitcast.me, f32[1024,512]{1,0:T(8,128)} %left.19, f32[512,4096]{1,0:T(8,128)} %right.19, f32[256,128,128]{2,1,0:T(8,128)} %child.19), custom_call_target="tpu_custom_call" | custom-call | flops 3221225472 | bytes 12845056 | tf_op jit(solution)/shard_map/pallas_call | solution.py:66
  61.4 40.5 %collective-permute-done.6.tiles = f32[4,128,128]{2,1,0:T(8,128)S(1)} collective-permute-done((f32[4,128,128]{2,1,0:T(8,128)S(1)}, f32[4,128,128]{2,1,0:T(8,128)S(1)}, u32[]{:S(2)}, u32[]{:S(2)}) %collective-permute-start.6) | collective-permute-done | bytes 262176 | tf_op jit(solution)/shard_map/ppermute | solution.py:302
  101.9 0.0 collective-permute-start.2
  101.9 0.0 collective-permute-done.5.tiles
  101.9 3.8 %collective-permute-start.1 = (f32[32,128,128]{2,1,0:T(8,128)}, f32[32,128,128]{2,1,0:T(8,128)}, u32[]{:S(2)}, u32[]{:S(2)}) collective-permute-start(f32[32,128,128]{2,1,0:T(8,128)} %shard_map.56), channel_id=1, source_target_pairs={{0,5},{1,4},{2,7},{3,6},{4,1},{5,0},{6,3},{7,2},{8,13},{9,12},{10,... | collective-permute-start | bytes 6291464 | tf_op jit(solution)/shard_map/ppermute | solution.py:302
  105.6 13.3 %shard_map.72 = f32[26,128,128]{2,1,0:T(8,128)} custom-call(s32[2,32]{1,0:T(2,128)} %labels.39, s32[1]{0:T(128)} %bitcast.me, f32[1024,512]{1,0:T(8,128)} %left.19, f32[512,4096]{1,0:T(8,128)} %right.19, f32[256,128,128]{2,1,0:T(8,128)} %child.19), custom_call_target="tpu_custom_call" | custom-call | flops 2617245696 | bytes 10485760 | tf_op jit(solution)/shard_map/pallas_call | solution.py:66
  118.9 0.0 collective-permute-done.7.tiles
  118.9 0.0 collective-permute-start.8
  118.9 4.8 %shard_map.55 = f32[6,128,128]{2,1,0:T(8,128)} custom-call(s32[2,32]{1,0:T(2,128)} %labels.39, s32[1]{0:T(128)} %bitcast.me, f32[1024,512]{1,0:T(8,128)} %left.19, f32[512,4096]{1,0:T(8,128)} %right.19, f32[256,128,128]{2,1,0:T(8,128)} %child.19), custom_call_target="tpu_custom_call" | custom-call | flops 603979776 | bytes 2621440 | tf_op jit(solution)/shard_map/pallas_call | solution.py:66
  123.8 0.0 collective-permute-done.4.tiles
  123.8 27.7 %collective-permute-start = (f32[6,128,128]{2,1,0:T(8,128)}, f32[6,128,128]{2,1,0:T(8,128)S(1)}, u32[]{:S(2)}, u32[]{:S(2)}) collective-permute-start(f32[6,128,128]{2,1,0:T(8,128)} %shard_map.55), channel_id=1, source_target_pairs={{0,7},{1,6},{2,5},{3,4},{4,3},{5,2},{6,1},{7,0},{8,15},{9,14},{10,... | collective-permute-start | bytes 1179656 | tf_op jit(solution)/shard_map/ppermute | solution.py:302
  151.4 8.9 %shard_map.63.tiles = f32[32,128,128]{2,1,0:T(8,128)} custom-call(s32[2,32]{1,0:T(2,128)} %labels.39, s32[1]{0:T(128)} %bitcast.me, f32[1024,512]{1,0:T(8,128)} %left.19, f32[512,4096]{1,0:T(8,128)} %right.19, f32[256,128,128]{2,1,0:T(8,128)} %child.19), custom_call_target="tpu_custom_call" | custom-call | flops 3221225472 | bytes 12845056 | tf_op jit(solution)/shard_map/pallas_call | solution.py:66
  160.3 0.0 copy-start
  160.3 16.1 %start_front.1.front_in = f32[288,128,128]{2,1,0:T(8,128)} custom-call(s32[2,32]{1,0:T(2,128)} %labels.39, s32[1]{0:T(128)} %bitcast.me, f32[288,128,128]{2,1,0:T(8,128)} %own.1, f32[32,128,128]{2,1,0:T(8,128)} %shard_map.63.tiles), custom_call_target="tpu_custom_call" | custom-call | tf_op jit(solution)/shard_map/start_front/pallas_call | solution.py:149
  176.4 0.0 copy-done
  176.4 5.0 %shard_map.64.front_in = f32[288,128,128]{2,1,0:T(8,128)} custom-call(s32[2,32]{1,0:T(2,128)S(1)} %copy-done, s32[1]{0:T(128)} %bitcast.me, f32[32,128,128]{2,1,0:T(8,128)} %collective-permute-done.7.tiles, f32[288,128,128]{2,1,0:T(8,128)} %start_front.1.front_in, s32[2,32]{1,0:T(2,128)S(1)} %copy-done), custom_call_target="tpu_custom_call", output_to_operand_aliasing={{}: (3, {})} | custom-call | tf_op jit(solution)/shard_map/pallas_call | solution.py:202
  181.4 2.3 shard_map.65.front_in
  183.7 4.8 %shard_map.66.front_in = f32[288,128,128]{2,1,0:T(8,128)} custom-call(s32[2,32]{1,0:T(2,128)S(1)} %copy-done, s32[1]{0:T(128)} %bitcast.me, f32[28,128,128]{2,1,0:T(8,128)} %collective-permute-done.5.tiles, f32[288,128,128]{2,1,0:T(8,128)} %shard_map.65.front_in, s32[2,32]{1,0:T(2,128)S(1)} %copy-done), custom_call_target="tpu_custom_call", output_to_operand_aliasing={{}: (3, {})} | custom-call | tf_op jit(solution)/shard_map/pallas_call | solution.py:202
  188.5 5.0 %shard_map.67.front_in = f32[288,128,128]{2,1,0:T(8,128)} custom-call(s32[2,32]{1,0:T(2,128)S(1)} %copy-done, s32[1]{0:T(128)} %bitcast.me, f32[32,128,128]{2,1,0:T(8,128)} %collective-permute-done.4.tiles, f32[288,128,128]{2,1,0:T(8,128)} %shard_map.66.front_in, s32[2,32]{1,0:T(2,128)S(1)} %copy-done), custom_call_target="tpu_custom_call", output_to_operand_aliasing={{}: (3, {})} | custom-call | tf_op jit(solution)/shard_map/pallas_call | solution.py:202
  193.5 0.0 collective-permute-done.3.tiles
  193.5 5.0 %shard_map.68.front_in = f32[288,128,128]{2,1,0:T(8,128)} custom-call(s32[2,32]{1,0:T(2,128)S(1)} %copy-done, s32[1]{0:T(128)} %bitcast.me, f32[32,128,128]{2,1,0:T(8,128)} %collective-permute-done.3.tiles, f32[288,128,128]{2,1,0:T(8,128)} %shard_map.67.front_in, s32[2,32]{1,0:T(2,128)S(1)} %copy-done), custom_call_target="tpu_custom_call", output_to_operand_aliasing={{}: (3, {})} | custom-call | tf_op jit(solution)/shard_map/pallas_call | solution.py:202
  198.5 0.0 collective-permute-done.2.tiles
  198.6 5.0 %shard_map.69.front_in = f32[288,128,128]{2,1,0:T(8,128)} custom-call(s32[2,32]{1,0:T(2,128)S(1)} %copy-done, s32[1]{0:T(128)} %bitcast.me, f32[32,128,128]{2,1,0:T(8,128)} %collective-permute-done.2.tiles, f32[288,128,128]{2,1,0:T(8,128)} %shard_map.68.front_in, s32[2,32]{1,0:T(2,128)S(1)} %copy-done), custom_call_target="tpu_custom_call", output_to_operand_aliasing={{}: (3, {})} | custom-call | tf_op jit(solution)/shard_map/pallas_call | solution.py:202
  203.6 122.5 %collective-permute-done.1.tiles = f32[32,128,128]{2,1,0:T(8,128)} collective-permute-done((f32[32,128,128]{2,1,0:T(8,128)}, f32[32,128,128]{2,1,0:T(8,128)}, u32[]{:S(2)}, u32[]{:S(2)}) %collective-permute-start.1) | collective-permute-done | bytes 2097184 | tf_op jit(solution)/shard_map/ppermute | solution.py:302
  326.1 5.0 %shard_map.70.front.front_in = f32[288,128,128]{2,1,0:T(8,128)} custom-call(s32[2,32]{1,0:T(2,128)S(1)} %copy-done, s32[1]{0:T(128)} %bitcast.me, f32[32,128,128]{2,1,0:T(8,128)} %collective-permute-done.1.tiles, f32[288,128,128]{2,1,0:T(8,128)} %shard_map.69.front_in, s32[2,32]{1,0:T(2,128)S(1)} %copy-done), custom_call_target="tpu_custom_call", output_to_operand_aliasing={{}: (3, {})} | custom-call | tf_op jit(solution)/shard_map/pallas_call | solution.py:202
  331.1 1.6 shard_map.71.after.old
  332.7 34.5 %collective-permute-done.8.tiles = f32[26,128,128]{2,1,0:T(8,128)} collective-permute-done((f32[26,128,128]{2,1,0:T(8,128)}, f32[26,128,128]{2,1,0:T(8,128)}, u32[]{:S(2)}, u32[]{:S(2)}) %collective-permute-start.8) | collective-permute-done | bytes 1703968 | tf_op jit(solution)/shard_map/ppermute | solution.py:302
  367.2 4.6 %shard_map.73.front_in = f32[288,128,128]{2,1,0:T(8,128)} custom-call(s32[2,32]{1,0:T(2,128)S(1)} %copy-done, s32[1]{0:T(128)} %bitcast.me, f32[26,128,128]{2,1,0:T(8,128)} %collective-permute-done.8.tiles, f32[288,128,128]{2,1,0:T(8,128)} %shard_map.70.front.front_in, f32[6,128,128]{2,1,0:T(8,128)S(1)} %shard_map.71.after.old), custom_call_target="tpu_custom_call", output_to_operand_aliasing={{}: (3, {})} | custom-call | tf_op jit(solution)/shard_map/pallas_call | solution.py:202
  371.9 2.0 collective-permute-done.tiles
  373.8 1.4 shard_map.74
Async XLA Ops:
  9.9 92.0 %collective-permute-start.5 = (f32[28,128,128]{2,1,0:T(8,128)}, f32[28,128,128]{2,1,0:T(8,128)}, u32[]{:S(2)}, u32[]{:S(2)}) collective-permute-start(f32[28,128,128]{2,1,0:T(8,128)} %shard_map.60), channel_id=1, source_target_pairs={{0,6},{1,7},{2,4},{3,5},{4,2},{5,3},{6,0},{7,1},{8,14},{9,15},{10,... | collective-permute-start | bytes 5505032 | tf_op jit(solution)/shard_map/ppermute | solution.py:302
  20.1 98.8 %collective-permute-start.7 = (f32[32,128,128]{2,1,0:T(8,128)}, f32[32,128,128]{2,1,0:T(8,128)}, u32[]{:S(2)}, u32[]{:S(2)}) collective-permute-start(f32[32,128,128]{2,1,0:T(8,128)} %shard_map.62), channel_id=1, source_target_pairs={{0,1},{1,0},{2,3},{3,2},{4,5},{5,4},{6,7},{7,6},{8,9},{9,8},{10,11... | collective-permute-start | bytes 6291464 | tf_op jit(solution)/shard_map/ppermute | solution.py:302
  23.5 78.3 %collective-permute-start.6 = (f32[4,128,128]{2,1,0:T(8,128)S(1)}, f32[4,128,128]{2,1,0:T(8,128)S(1)}, u32[]{:S(2)}, u32[]{:S(2)}) collective-permute-start(f32[4,128,128]{2,1,0:T(8,128)S(1)} %shard_map.61), channel_id=1, source_target_pairs={{0,6},{1,7},{2,4},{3,5},{4,2},{5,3},{6,0},{7,1},{8,14},{9,15},{10,... | collective-permute-start | bytes 786440 | tf_op jit(solution)/shard_map/ppermute | solution.py:302
  32.7 91.1 %collective-permute-start.4 = (f32[32,128,128]{2,1,0:T(8,128)}, f32[32,128,128]{2,1,0:T(8,128)}, u32[]{:S(2)}, u32[]{:S(2)}) collective-permute-start(f32[32,128,128]{2,1,0:T(8,128)} %shard_map.59), channel_id=1, source_target_pairs={{0,2},{1,3},{2,0},{3,1},{4,6},{5,7},{6,4},{7,5},{8,10},{9,11},{10,... | collective-permute-start | bytes 6291464 | tf_op jit(solution)/shard_map/ppermute | solution.py:302
  43.6 149.9 %collective-permute-start.3 = (f32[32,128,128]{2,1,0:T(8,128)}, f32[32,128,128]{2,1,0:T(8,128)}, u32[]{:S(2)}, u32[]{:S(2)}) collective-permute-start(f32[32,128,128]{2,1,0:T(8,128)} %shard_map.58), channel_id=1, source_target_pairs={{0,3},{1,2},{2,1},{3,0},{4,7},{5,6},{6,5},{7,4},{8,11},{9,10},{10,... | collective-permute-start | bytes 6291464 | tf_op jit(solution)/shard_map/ppermute | solution.py:302
  101.9 96.7 %collective-permute-start.2 = (f32[32,128,128]{2,1,0:T(8,128)}, f32[32,128,128]{2,1,0:T(8,128)}, u32[]{:S(2)}, u32[]{:S(2)}) collective-permute-start(f32[32,128,128]{2,1,0:T(8,128)} %shard_map.57), channel_id=1, source_target_pairs={{0,4},{1,5},{2,6},{3,7},{4,0},{5,1},{6,2},{7,3},{8,12},{9,13},{10,... | collective-permute-start | bytes 6291464 | tf_op jit(solution)/shard_map/ppermute | solution.py:302
  101.9 224.2 %collective-permute-start.1 = (f32[32,128,128]{2,1,0:T(8,128)}, f32[32,128,128]{2,1,0:T(8,128)}, u32[]{:S(2)}, u32[]{:S(2)}) collective-permute-start(f32[32,128,128]{2,1,0:T(8,128)} %shard_map.56), channel_id=1, source_target_pairs={{0,5},{1,4},{2,7},{3,6},{4,1},{5,0},{6,3},{7,2},{8,13},{9,12},{10,... | collective-permute-start | bytes 6291464 | tf_op jit(solution)/shard_map/ppermute | solution.py:302
  118.9 248.3 %collective-permute-start.8 = (f32[26,128,128]{2,1,0:T(8,128)}, f32[26,128,128]{2,1,0:T(8,128)}, u32[]{:S(2)}, u32[]{:S(2)}) collective-permute-start(f32[26,128,128]{2,1,0:T(8,128)} %shard_map.72), channel_id=1, source_target_pairs={{0,7},{1,6},{2,5},{3,4},{4,3},{5,2},{6,1},{7,0},{8,15},{9,14},{10,... | collective-permute-start | bytes 5111816 | tf_op jit(solution)/shard_map/ppermute | solution.py:302
  123.8 250.1 %collective-permute-start = (f32[6,128,128]{2,1,0:T(8,128)}, f32[6,128,128]{2,1,0:T(8,128)S(1)}, u32[]{:S(2)}, u32[]{:S(2)}) collective-permute-start(f32[6,128,128]{2,1,0:T(8,128)} %shard_map.55), channel_id=1, source_target_pairs={{0,7},{1,6},{2,5},{3,4},{4,3},{5,2},{6,1},{7,0},{8,15},{9,14},{10,... | collective-permute-start | bytes 1179656 | tf_op jit(solution)/shard_map/ppermute | solution.py:302
  160.3 16.1 %copy-start = (s32[2,32]{1,0:T(2,128)S(1)}, s32[2,32]{1,0:T(2,128)}, u32[]{:S(2)}) copy-start(s32[2,32]{1,0:T(2,128)} %labels.39) | copy-start | bytes 772

commit v4 on v3

--- a/solution.py
+++ b/solution.py
@@ -14,7 +14,11 @@
 CGR = 4
 PR = 8
 MIB = 1024 * 1024
-VMEM_LIMIT = int(62.5 * MIB)
+VMEM_LIMIT = 24 * MIB
+
+
+def in_hbm(x):
+    return pltpu.with_memory_space_constraint(x, pltpu.HBM)
 
 
 def row_for(labels, me, ncd, dest):
@@ -73,7 +77,7 @@
             transcendentals=0,
         ),
         compiler_params=pltpu.CompilerParams(vmem_limit_bytes=VMEM_LIMIT),
-    )(labels, me, l_slab, u_slab, child_tiles)
+    )(in_hbm(labels), me, *(in_hbm(x) for x in (l_slab, u_slab, child_tiles)))
 
 
 def first_kernel(ncd, step, table, left, right, child, out, labels, rows, columns, sems):
@@ -119,7 +123,7 @@
             pltpu.SemaphoreType.DMA((4,)),
         ],
         compiler_params=pltpu.CompilerParams(vmem_limit_bytes=8 * MIB),
-    )(*(pltpu.with_memory_space_constraint(x, pltpu.HBM) for x in arrays))
+    )(*(in_hbm(x) for x in arrays))
 
 
 def start_front_kernel(ncd, labels, me, own, tiles, out):
@@ -152,7 +156,7 @@
         out_shape=jax.ShapeDtypeStruct(own.shape, own.dtype),
         compiler_params=pltpu.CompilerParams(vmem_limit_bytes=VMEM_LIMIT),
         name="start_front",
-    )(labels, me, own, tiles)
+    )(labels, me, in_hbm(own), tiles)
 
 
 def each(count, action):
@@ -239,7 +243,7 @@
         grid_spec=grid_spec,
         out_shape=jax.ShapeDtypeStruct(shape, jnp.float32),
         compiler_params=pltpu.CompilerParams(vmem_limit_bytes=50 * MIB),
-    )(labels, me, front)
+    )(labels, me, in_hbm(front))
 
 
 def put(labels, me, tiles, old, front, ncd, step, first):
@@ -267,14 +271,14 @@
     (6, 4, 28, 4),
     (4, 0, 32, 8),
     (5, 0, 32, 8),
-    (7, 0, 26, 2),
-    (7, 26, 6, 2),
+    (7, 0, 28, 4),
+    (7, 28, 4, 4),
     (1, 0, 32, 8),
     (2, 0, 32, 8),
     (3, 0, 32, 8),
 )
 ADDS = ((1, 0), (6, 0), (6, 4), (2, 0), (3, 0), (4, 0), (5, 0), (7, 0))
-LAST = (7, 26)
+LAST = (7, 28)
 
 
 def body_rows(child_tiles, l_slab, u_slab, parent_own_entries, parent_label):

time: 377 us -> 376 us (level)
  the two profiles are of different devices: /device:TPU:9 before, /device:TPU:13 now
where the time goes in v4:
time: 376 us; the launch traced here: 374 us
  waiting for transfers between devices  214 us (57%)
  Pallas kernels  117 us (31%)
  starting transfers between devices  43 us (11%)
    ppermute x9, waiting for transfers between devices, body_rows(): arrived[step, first] = lax.ppermute(tiles, 'dev', pairs)  214 us
    pallas_call x9, Pallas kernels, stripe(): pl.pallas_call(stripe_kernel, grid_spec=grid_spec, out_shape=jax.ShapeDty...  70.3 us
    ppermute x9, starting transfers between devices, body_rows(): arrived[step, first] = lax.ppermute(tiles, 'dev', pairs)  43 us
    pallas_call x8, Pallas kernels, extend(): pl.pallas_call(functools.partial(extend_kernel, ncd, step, first), grid_s...  26.6 us
    pallas_call x1, Pallas kernels, start_front(): pl.pallas_call(functools.partial(start_front_kernel, ncd), grid_spec=grid...  14.6 us
  transfers between devices with their start and end apart: 9, of which 5 were waited for; matrix products, arithmetic and copies ran while one was open for 0% of the time, Pallas kernels for 28%

profile of v4, /device:TPU:13, one launch (start us, length us, event | category | flops | bytes accessed | tf_op | source)
XLA Modules:
  0.0 374.1 jit_solution(11336713342783887991)
XLA Ops:
  0.0 9.3 %shard_map.60 = f32[28,128,128]{2,1,0:T(8,128)S(1)} custom-call(s32[2,32]{1,0:T(2,128)} %labels.39, s32[1]{0:T(128)} %bitcast.me, f32[1024,512]{1,0:T(8,128)} %left.19, f32[512,4096]{1,0:T(8,128)} %right.19, f32[256,128,128]{2,1,0:T(8,128)} %child.19), custom_call_target="tpu_custom_call" | custom-call | flops 2818572288 | bytes 11272192 | tf_op jit(solution)/shard_map/pallas_call | solution.py:70
  9.3 1.4 collective-permute-start.5
  10.7 8.2 %shard_map.62 = f32[32,128,128]{2,1,0:T(8,128)S(1)} custom-call(s32[2,32]{1,0:T(2,128)} %labels.39, s32[1]{0:T(128)} %bitcast.me, f32[1024,512]{1,0:T(8,128)} %left.19, f32[512,4096]{1,0:T(8,128)} %right.19, f32[256,128,128]{2,1,0:T(8,128)} %child.19), custom_call_target="tpu_custom_call" | custom-call | flops 3221225472 | bytes 12845056 | tf_op jit(solution)/shard_map/pallas_call | solution.py:70
  18.8 1.0 collective-permute-start.7
  19.9 2.5 shard_map.61
  22.3 0.2 collective-permute-start.6
  22.6 8.2 %shard_map.59 = f32[32,128,128]{2,1,0:T(8,128)S(1)} custom-call(s32[2,32]{1,0:T(2,128)} %labels.39, s32[1]{0:T(128)} %bitcast.me, f32[1024,512]{1,0:T(8,128)} %left.19, f32[512,4096]{1,0:T(8,128)} %right.19, f32[256,128,128]{2,1,0:T(8,128)} %child.19), custom_call_target="tpu_custom_call" | custom-call | flops 3221225472 | bytes 12845056 | tf_op jit(solution)/shard_map/pallas_call | solution.py:70
  30.8 2.1 collective-permute-start.4
  32.9 8.2 %shard_map.58 = f32[32,128,128]{2,1,0:T(8,128)S(1)} custom-call(s32[2,32]{1,0:T(2,128)} %labels.39, s32[1]{0:T(128)} %bitcast.me, f32[1024,512]{1,0:T(8,128)} %left.19, f32[512,4096]{1,0:T(8,128)} %right.19, f32[256,128,128]{2,1,0:T(8,128)} %child.19), custom_call_target="tpu_custom_call" | custom-call | flops 3221225472 | bytes 12845056 | tf_op jit(solution)/shard_map/pallas_call | solution.py:70
  41.0 0.2 collective-permute-start.3
  41.2 8.2 %shard_map.57 = f32[32,128,128]{2,1,0:T(8,128)S(1)} custom-call(s32[2,32]{1,0:T(2,128)} %labels.39, s32[1]{0:T(128)} %bitcast.me, f32[1024,512]{1,0:T(8,128)} %left.19, f32[512,4096]{1,0:T(8,128)} %right.19, f32[256,128,128]{2,1,0:T(8,128)} %child.19), custom_call_target="tpu_custom_call" | custom-call | flops 3221225472 | bytes 12845056 | tf_op jit(solution)/shard_map/pallas_call | solution.py:70
  49.4 8.2 %shard_map.56 = f32[32,128,128]{2,1,0:T(8,128)S(1)} custom-call(s32[2,32]{1,0:T(2,128)} %labels.39, s32[1]{0:T(128)} %bitcast.me, f32[1024,512]{1,0:T(8,128)} %left.19, f32[512,4096]{1,0:T(8,128)} %right.19, f32[256,128,128]{2,1,0:T(8,128)} %child.19), custom_call_target="tpu_custom_call" | custom-call | flops 3221225472 | bytes 12845056 | tf_op jit(solution)/shard_map/pallas_call | solution.py:70
  57.6 43.4 %collective-permute-done.6.tiles = f32[4,128,128]{2,1,0:T(8,128)S(1)} collective-permute-done((f32[4,128,128]{2,1,0:T(8,128)S(1)}, f32[4,128,128]{2,1,0:T(8,128)S(1)}, u32[]{:S(2)}, u32[]{:S(2)}) %collective-permute-start.6) | collective-permute-done | bytes 262176 | tf_op jit(solution)/shard_map/ppermute | solution.py:306
  101.0 0.0 collective-permute-start.2
  101.0 0.0 collective-permute-done.5.tiles
  101.0 3.9 %collective-permute-start.1 = (f32[32,128,128]{2,1,0:T(8,128)S(1)}, f32[32,128,128]{2,1,0:T(8,128)S(1)}, u32[]{:S(2)}, u32[]{:S(2)}) collective-permute-start(f32[32,128,128]{2,1,0:T(8,128)S(1)} %shard_map.56), channel_id=1, source_target_pairs={{0,5},{1,4},{2,7},{3,6},{4,1},{5,0},{6,3},{7,2},{8,13},{9,12},{10,... | collective-permute-start | bytes 6291464 | tf_op jit(solution)/shard_map/ppermute | solution.py:306
  104.9 9.3 %shard_map.72 = f32[28,128,128]{2,1,0:T(8,128)S(1)} custom-call(s32[2,32]{1,0:T(2,128)} %labels.39, s32[1]{0:T(128)} %bitcast.me, f32[1024,512]{1,0:T(8,128)} %left.19, f32[512,4096]{1,0:T(8,128)} %right.19, f32[256,128,128]{2,1,0:T(8,128)} %child.19), custom_call_target="tpu_custom_call" | custom-call | flops 2818572288 | bytes 11272192 | tf_op jit(solution)/shard_map/pallas_call | solution.py:70
  114.2 0.0 collective-permute-done.7.tiles
  114.2 0.1 collective-permute-start.8
  114.3 2.7 shard_map.55
  117.0 0.0 copy-start
  117.0 0.0 collective-permute-done.4.tiles
  117.0 34.1 %collective-permute-start = (f32[4,128,128]{2,1,0:T(8,128)S(1)}, f32[4,128,128]{2,1,0:T(8,128)S(1)}, u32[]{:S(2)}, u32[]{:S(2)}) collective-permute-start(f32[4,128,128]{2,1,0:T(8,128)S(1)} %shard_map.55), channel_id=1, source_target_pairs={{0,7},{1,6},{2,5},{3,4},{4,3},{5,2},{6,1},{7,0},{8,15},{9,14},{10,... | collective-permute-start | bytes 786440 | tf_op jit(solution)/shard_map/ppermute | solution.py:306
  151.1 8.2 %shard_map.63.tiles = f32[32,128,128]{2,1,0:T(8,128)S(1)} custom-call(s32[2,32]{1,0:T(2,128)} %labels.39, s32[1]{0:T(128)} %bitcast.me, f32[1024,512]{1,0:T(8,128)} %left.19, f32[512,4096]{1,0:T(8,128)} %right.19, f32[256,128,128]{2,1,0:T(8,128)} %child.19), custom_call_target="tpu_custom_call" | custom-call | flops 3221225472 | bytes 12845056 | tf_op jit(solution)/shard_map/pallas_call | solution.py:70
  159.3 0.0 copy-done
  159.3 14.6 %start_front.1.front_in = f32[288,128,128]{2,1,0:T(8,128)} custom-call(s32[2,32]{1,0:T(2,128)S(1)} %copy-done, s32[1]{0:T(128)} %bitcast.me, f32[288,128,128]{2,1,0:T(8,128)} %own.1, f32[32,128,128]{2,1,0:T(8,128)S(1)} %shard_map.63.tiles), custom_call_target="tpu_custom_call" | custom-call | tf_op jit(solution)/shard_map/start_front/pallas_call | solution.py:153
  173.9 3.5 shard_map.64.front_in
  177.4 2.3 shard_map.65.front_in
  179.7 3.4 shard_map.66.front_in
  183.1 3.5 shard_map.67.front_in
  186.6 4.7 %collective-permute-done.3.tiles = f32[32,128,128]{2,1,0:T(8,128)S(1)} collective-permute-done((f32[32,128,128]{2,1,0:T(8,128)S(1)}, f32[32,128,128]{2,1,0:T(8,128)S(1)}, u32[]{:S(2)}, u32[]{:S(2)}) %collective-permute-start.3) | collective-permute-done | bytes 2097184 | tf_op jit(solution)/shard_map/ppermute | solution.py:306
  191.3 3.5 shard_map.68.front_in
  194.8 0.0 collective-permute-done.2.tiles
  194.8 3.5 shard_map.69.front_in
  198.4 126.4 %collective-permute-done.1.tiles = f32[32,128,128]{2,1,0:T(8,128)S(1)} collective-permute-done((f32[32,128,128]{2,1,0:T(8,128)S(1)}, f32[32,128,128]{2,1,0:T(8,128)S(1)}, u32[]{:S(2)}, u32[]{:S(2)}) %collective-permute-start.1) | collective-permute-done | bytes 2097184 | tf_op jit(solution)/shard_map/ppermute | solution.py:306
  324.8 3.5 shard_map.70.front.front_in
  328.3 1.6 shard_map.71.after.old
  329.9 39.2 %collective-permute-done.8.tiles = f32[28,128,128]{2,1,0:T(8,128)S(1)} collective-permute-done((f32[28,128,128]{2,1,0:T(8,128)S(1)}, f32[28,128,128]{2,1,0:T(8,128)S(1)}, u32[]{:S(2)}, u32[]{:S(2)}) %collective-permute-start.8) | collective-permute-done | bytes 1835040 | tf_op jit(solution)/shard_map/ppermute | solution.py:306
  369.1 3.4 shard_map.73.front_in
  372.5 0.3 collective-permute-done.tiles
  372.8 1.3 shard_map.74
Async XLA Ops:
  9.3 91.7 %collective-permute-start.5 = (f32[28,128,128]{2,1,0:T(8,128)S(1)}, f32[28,128,128]{2,1,0:T(8,128)S(1)}, u32[]{:S(2)}, u32[]{:S(2)}) collective-permute-start(f32[28,128,128]{2,1,0:T(8,128)S(1)} %shard_map.60), channel_id=1, source_target_pairs={{0,6},{1,7},{2,4},{3,5},{4,2},{5,3},{6,0},{7,1},{8,14},{9,15},{10,... | collective-permute-start | bytes 5505032 | tf_op jit(solution)/shard_map/ppermute | solution.py:306
  18.8 95.3 %collective-permute-start.7 = (f32[32,128,128]{2,1,0:T(8,128)S(1)}, f32[32,128,128]{2,1,0:T(8,128)S(1)}, u32[]{:S(2)}, u32[]{:S(2)}) collective-permute-start(f32[32,128,128]{2,1,0:T(8,128)S(1)} %shard_map.62), channel_id=1, source_target_pairs={{0,1},{1,0},{2,3},{3,2},{4,5},{5,4},{6,7},{7,6},{8,9},{9,8},{10,11... | collective-permute-start | bytes 6291464 | tf_op jit(solution)/shard_map/ppermute | solution.py:306
  22.3 78.7 %collective-permute-start.6 = (f32[4,128,128]{2,1,0:T(8,128)S(1)}, f32[4,128,128]{2,1,0:T(8,128)S(1)}, u32[]{:S(2)}, u32[]{:S(2)}) collective-permute-start(f32[4,128,128]{2,1,0:T(8,128)S(1)} %shard_map.61), channel_id=1, source_target_pairs={{0,6},{1,7},{2,4},{3,5},{4,2},{5,3},{6,0},{7,1},{8,14},{9,15},{10,... | collective-permute-start | bytes 786440 | tf_op jit(solution)/shard_map/ppermute | solution.py:306
  30.8 86.2 %collective-permute-start.4 = (f32[32,128,128]{2,1,0:T(8,128)S(1)}, f32[32,128,128]{2,1,0:T(8,128)S(1)}, u32[]{:S(2)}, u32[]{:S(2)}) collective-permute-start(f32[32,128,128]{2,1,0:T(8,128)S(1)} %shard_map.59), channel_id=1, source_target_pairs={{0,2},{1,3},{2,0},{3,1},{4,6},{5,7},{6,4},{7,5},{8,10},{9,11},{10,... | collective-permute-start | bytes 6291464 | tf_op jit(solution)/shard_map/ppermute | solution.py:306
  41.0 150.3 %collective-permute-start.3 = (f32[32,128,128]{2,1,0:T(8,128)S(1)}, f32[32,128,128]{2,1,0:T(8,128)S(1)}, u32[]{:S(2)}, u32[]{:S(2)}) collective-permute-start(f32[32,128,128]{2,1,0:T(8,128)S(1)} %shard_map.58), channel_id=1, source_target_pairs={{0,3},{1,2},{2,1},{3,0},{4,7},{5,6},{6,5},{7,4},{8,11},{9,10},{10,... | collective-permute-start | bytes 6291464 | tf_op jit(solution)/shard_map/ppermute | solution.py:306
  101.0 93.8 %collective-permute-start.2 = (f32[32,128,128]{2,1,0:T(8,128)S(1)}, f32[32,128,128]{2,1,0:T(8,128)S(1)}, u32[]{:S(2)}, u32[]{:S(2)}) collective-permute-start(f32[32,128,128]{2,1,0:T(8,128)S(1)} %shard_map.57), channel_id=1, source_target_pairs={{0,4},{1,5},{2,6},{3,7},{4,0},{5,1},{6,2},{7,3},{8,12},{9,13},{10,... | collective-permute-start | bytes 6291464 | tf_op jit(solution)/shard_map/ppermute | solution.py:306
  101.0 223.8 %collective-permute-start.1 = (f32[32,128,128]{2,1,0:T(8,128)S(1)}, f32[32,128,128]{2,1,0:T(8,128)S(1)}, u32[]{:S(2)}, u32[]{:S(2)}) collective-permute-start(f32[32,128,128]{2,1,0:T(8,128)S(1)} %shard_map.56), channel_id=1, source_target_pairs={{0,5},{1,4},{2,7},{3,6},{4,1},{5,0},{6,3},{7,2},{8,13},{9,12},{10,... | collective-permute-start | bytes 6291464 | tf_op jit(solution)/shard_map/ppermute | solution.py:306
  114.2 254.9 %collective-permute-start.8 = (f32[28,128,128]{2,1,0:T(8,128)S(1)}, f32[28,128,128]{2,1,0:T(8,128)S(1)}, u32[]{:S(2)}, u32[]{:S(2)}) collective-permute-start(f32[28,128,128]{2,1,0:T(8,128)S(1)} %shard_map.72), channel_id=1, source_target_pairs={{0,7},{1,6},{2,5},{3,4},{4,3},{5,2},{6,1},{7,0},{8,15},{9,14},{10,... | collective-permute-start | bytes 5505032 | tf_op jit(solution)/shard_map/ppermute | solution.py:306
  117.0 42.3 %copy-start = (s32[2,32]{1,0:T(2,128)S(1)}, s32[2,32]{1,0:T(2,128)}, u32[]{:S(2)}) copy-start(s32[2,32]{1,0:T(2,128)} %labels.39) | copy-start | bytes 772
  117.0 255.8 %collective-permute-start = (f32[4,128,128]{2,1,0:T(8,128)S(1)}, f32[4,128,128]{2,1,0:T(8,128)S(1)}, u32[]{:S(2)}, u32[]{:S(2)}) collective-permute-start(f32[4,128,128]{2,1,0:T(8,128)S(1)} %shard_map.55), channel_id=1, source_target_pairs={{0,7},{1,6},{2,5},{3,4},{4,3},{5,2},{6,1},{7,0},{8,15},{9,14},{10,... | collective-permute-start | bytes 786440 | tf_op jit(solution)/shard_map/ppermute | solution.py:306

commit v5 on v4

--- a/solution.py
+++ b/solution.py
@@ -267,8 +267,9 @@
 
 
 SENDS = (
-    (6, 0, 4, 4),
-    (6, 4, 28, 4),
+    (6, 0, 2, 2),
+    (6, 2, 6, 2),
+    (6, 8, 24, 8),
     (4, 0, 32, 8),
     (5, 0, 32, 8),
     (7, 0, 28, 4),
@@ -277,7 +278,7 @@
     (2, 0, 32, 8),
     (3, 0, 32, 8),
 )
-ADDS = ((1, 0), (6, 0), (6, 4), (2, 0), (3, 0), (4, 0), (5, 0), (7, 0))
+ADDS = ((1, 0), (6, 0), (6, 2), (6, 8), (2, 0), (3, 0), (4, 0), (5, 0), (7, 0))
 LAST = (7, 28)
 
 

time: 376 us -> 383 us (1.019)
  the two profiles are of different devices: /device:TPU:13 before, /device:TPU:15 now
where the time goes in v5:
time: 383 us; the launch traced here: 381 us
  waiting for transfers between devices  215 us (56%)
  Pallas kernels  121 us (32%)
  starting transfers between devices  44.9 us (12%)
    ppermute x10, waiting for transfers between devices, body_rows(): arrived[step, first] = lax.ppermute(tiles, 'dev', pairs)  215 us
    pallas_call x10, Pallas kernels, stripe(): pl.pallas_call(stripe_kernel, grid_spec=grid_spec, out_shape=jax.ShapeDty...  72.3 us
    ppermute x10, starting transfers between devices, body_rows(): arrived[step, first] = lax.ppermute(tiles, 'dev', pairs)  44.9 us
    pallas_call x9, Pallas kernels, extend(): pl.pallas_call(functools.partial(extend_kernel, ncd, step, first), grid_s...  28.7 us
    pallas_call x1, Pallas kernels, start_front(): pl.pallas_call(functools.partial(start_front_kernel, ncd), grid_spec=grid...  15.1 us
  transfers between devices with their start and end apart: 10, of which 6 were waited for; matrix products, arithmetic and copies ran while one was open for 0% of the time, Pallas kernels for 29%

profile of v5, /device:TPU:15, one launch (start us, length us, event | category | flops | bytes accessed | tf_op | source)
XLA Modules:
  0.0 381.3 jit_solution(17432653217426476172)
XLA Ops:
  0.0 8.2 %shard_map.63 = f32[32,128,128]{2,1,0:T(8,128)S(1)} custom-call(s32[2,32]{1,0:T(2,128)} %labels.43, s32[1]{0:T(128)} %bitcast.me, f32[1024,512]{1,0:T(8,128)} %left.21, f32[512,4096]{1,0:T(8,128)} %right.21, f32[256,128,128]{2,1,0:T(8,128)} %child.21), custom_call_target="tpu_custom_call" | custom-call | flops 3221225472 | bytes 12845056 | tf_op jit(solution)/shard_map/pallas_call | solution.py:70
  8.2 0.7 collective-permute-start.8
  8.9 6.8 %shard_map.60 = f32[24,128,128]{2,1,0:T(8,128)S(1)} custom-call(s32[2,32]{1,0:T(2,128)} %labels.43, s32[1]{0:T(128)} %bitcast.me, f32[1024,512]{1,0:T(8,128)} %left.21, f32[512,4096]{1,0:T(8,128)} %right.21, f32[256,128,128]{2,1,0:T(8,128)} %child.21), custom_call_target="tpu_custom_call" | custom-call | flops 2415919104 | bytes 9699328 | tf_op jit(solution)/shard_map/pallas_call | solution.py:70
  15.7 1.4 collective-permute-start.5
  17.1 2.2 shard_map.62
  19.3 0.2 collective-permute-start.7
  19.5 4.3 %shard_map.61 = f32[6,128,128]{2,1,0:T(8,128)S(1)} custom-call(s32[2,32]{1,0:T(2,128)} %labels.43, s32[1]{0:T(128)} %bitcast.me, f32[1024,512]{1,0:T(8,128)} %left.21, f32[512,4096]{1,0:T(8,128)} %right.21, f32[256,128,128]{2,1,0:T(8,128)} %child.21), custom_call_target="tpu_custom_call" | custom-call | flops 603979776 | bytes 2621440 | tf_op jit(solution)/shard_map/pallas_call | solution.py:70
  23.8 1.4 collective-permute-start.6
  25.2 8.2 %shard_map.59 = f32[32,128,128]{2,1,0:T(8,128)S(1)} custom-call(s32[2,32]{1,0:T(2,128)} %labels.43, s32[1]{0:T(128)} %bitcast.me, f32[1024,512]{1,0:T(8,128)} %left.21, f32[512,4096]{1,0:T(8,128)} %right.21, f32[256,128,128]{2,1,0:T(8,128)} %child.21), custom_call_target="tpu_custom_call" | custom-call | flops 3221225472 | bytes 12845056 | tf_op jit(solution)/shard_map/pallas_call | solution.py:70
  33.4 4.1 %collective-permute-start.4 = (f32[32,128,128]{2,1,0:T(8,128)S(1)}, f32[32,128,128]{2,1,0:T(8,128)S(1)}, u32[]{:S(2)}, u32[]{:S(2)}) collective-permute-start(f32[32,128,128]{2,1,0:T(8,128)S(1)} %shard_map.59), channel_id=1, source_target_pairs={{0,2},{1,3},{2,0},{3,1},{4,6},{5,7},{6,4},{7,5},{8,10},{9,11},{10,... | collective-permute-start | bytes 6291464 | tf_op jit(solution)/shard_map/ppermute | solution.py:307
  37.4 8.2 %shard_map.58 = f32[32,128,128]{2,1,0:T(8,128)S(1)} custom-call(s32[2,32]{1,0:T(2,128)} %labels.43, s32[1]{0:T(128)} %bitcast.me, f32[1024,512]{1,0:T(8,128)} %left.21, f32[512,4096]{1,0:T(8,128)} %right.21, f32[256,128,128]{2,1,0:T(8,128)} %child.21), custom_call_target="tpu_custom_call" | custom-call | flops 3221225472 | bytes 12845056 | tf_op jit(solution)/shard_map/pallas_call | solution.py:70
  45.6 8.2 %shard_map.57 = f32[32,128,128]{2,1,0:T(8,128)S(1)} custom-call(s32[2,32]{1,0:T(2,128)} %labels.43, s32[1]{0:T(128)} %bitcast.me, f32[1024,512]{1,0:T(8,128)} %left.21, f32[512,4096]{1,0:T(8,128)} %right.21, f32[256,128,128]{2,1,0:T(8,128)} %child.21), custom_call_target="tpu_custom_call" | custom-call | flops 3221225472 | bytes 12845056 | tf_op jit(solution)/shard_map/pallas_call | solution.py:70
  53.8 8.2 %shard_map.56 = f32[32,128,128]{2,1,0:T(8,128)S(1)} custom-call(s32[2,32]{1,0:T(2,128)} %labels.43, s32[1]{0:T(128)} %bitcast.me, f32[1024,512]{1,0:T(8,128)} %left.21, f32[512,4096]{1,0:T(8,128)} %right.21, f32[256,128,128]{2,1,0:T(8,128)} %child.21), custom_call_target="tpu_custom_call" | custom-call | flops 3221225472 | bytes 12845056 | tf_op jit(solution)/shard_map/pallas_call | solution.py:70
  61.9 37.5 %collective-permute-done.7.tiles = f32[2,128,128]{2,1,0:T(8,128)S(1)} collective-permute-done((f32[2,128,128]{2,1,0:T(8,128)S(1)}, f32[2,128,128]{2,1,0:T(8,128)S(1)}, u32[]{:S(2)}, u32[]{:S(2)}) %collective-permute-start.7) | collective-permute-done | bytes 131104 | tf_op jit(solution)/shard_map/ppermute | solution.py:307
  99.4 0.0 collective-permute-start.3
  99.4 8.4 %collective-permute-done.6.tiles = f32[6,128,128]{2,1,0:T(8,128)S(1)} collective-permute-done((f32[6,128,128]{2,1,0:T(8,128)S(1)}, f32[6,128,128]{2,1,0:T(8,128)S(1)}, u32[]{:S(2)}, u32[]{:S(2)}) %collective-permute-start.6) | collective-permute-done | bytes 393248 | tf_op jit(solution)/shard_map/ppermute | solution.py:307
  107.9 0.0 collective-permute-start.2
  107.9 0.0 collective-permute-done.5.tiles
  107.9 3.4 collective-permute-start.1
  111.3 9.3 %shard_map.74 = f32[28,128,128]{2,1,0:T(8,128)S(1)} custom-call(s32[2,32]{1,0:T(2,128)} %labels.43, s32[1]{0:T(128)} %bitcast.me, f32[1024,512]{1,0:T(8,128)} %left.21, f32[512,4096]{1,0:T(8,128)} %right.21, f32[256,128,128]{2,1,0:T(8,128)} %child.21), custom_call_target="tpu_custom_call" | custom-call | flops 2818572288 | bytes 11272192 | tf_op jit(solution)/shard_map/pallas_call | solution.py:70
  120.6 0.0 collective-permute-done.8.tiles
  120.6 0.6 collective-permute-start.9
  121.2 2.7 shard_map.55
  123.9 0.0 copy-start
  123.9 0.0 collective-permute-done.4.tiles
  123.9 33.1 %collective-permute-start = (f32[4,128,128]{2,1,0:T(8,128)S(1)}, f32[4,128,128]{2,1,0:T(8,128)S(1)}, u32[]{:S(2)}, u32[]{:S(2)}) collective-permute-start(f32[4,128,128]{2,1,0:T(8,128)S(1)} %shard_map.55), channel_id=1, source_target_pairs={{0,7},{1,6},{2,5},{3,4},{4,3},{5,2},{6,1},{7,0},{8,15},{9,14},{10,... | collective-permute-start | bytes 786440 | tf_op jit(solution)/shard_map/ppermute | solution.py:307
  157.0 8.4 %shard_map.64.tiles = f32[32,128,128]{2,1,0:T(8,128)S(1)} custom-call(s32[2,32]{1,0:T(2,128)} %labels.43, s32[1]{0:T(128)} %bitcast.me, f32[1024,512]{1,0:T(8,128)} %left.21, f32[512,4096]{1,0:T(8,128)} %right.21, f32[256,128,128]{2,1,0:T(8,128)} %child.21), custom_call_target="tpu_custom_call" | custom-call | flops 3221225472 | bytes 12845056 | tf_op jit(solution)/shard_map/pallas_call | solution.py:70
  165.4 0.0 copy-done
  165.4 15.1 %start_front.1.front_in = f32[288,128,128]{2,1,0:T(8,128)} custom-call(s32[2,32]{1,0:T(2,128)S(1)} %copy-done, s32[1]{0:T(128)} %bitcast.me, f32[288,128,128]{2,1,0:T(8,128)} %own.1, f32[32,128,128]{2,1,0:T(8,128)S(1)} %shard_map.64.tiles), custom_call_target="tpu_custom_call" | custom-call | tf_op jit(solution)/shard_map/start_front/pallas_call | solution.py:153
  180.5 3.5 shard_map.65.front_in
  184.1 2.2 shard_map.66.front_in
  186.2 2.4 shard_map.67.front_in
  188.6 3.2 shard_map.68.front_in
  191.8 3.5 shard_map.69.front_in
  195.4 1.6 collective-permute-done.3.tiles
  197.0 3.5 shard_map.70.front_in
  200.5 0.0 collective-permute-done.2.tiles
  200.5 3.5 shard_map.71.front_in
  204.1 128.0 %collective-permute-done.1.tiles = f32[32,128,128]{2,1,0:T(8,128)S(1)} collective-permute-done((f32[32,128,128]{2,1,0:T(8,128)S(1)}, f32[32,128,128]{2,1,0:T(8,128)S(1)}, u32[]{:S(2)}, u32[]{:S(2)}) %collective-permute-start.1) | collective-permute-done | bytes 2097184 | tf_op jit(solution)/shard_map/ppermute | solution.py:307
  332.1 3.5 shard_map.72.front.front_in
  335.6 1.6 shard_map.73.after.old
  337.2 38.3 %collective-permute-done.9.tiles = f32[28,128,128]{2,1,0:T(8,128)S(1)} collective-permute-done((f32[28,128,128]{2,1,0:T(8,128)S(1)}, f32[28,128,128]{2,1,0:T(8,128)S(1)}, u32[]{:S(2)}, u32[]{:S(2)}) %collective-permute-start.9) | collective-permute-done | bytes 1835040 | tf_op jit(solution)/shard_map/ppermute | solution.py:307
  375.5 3.4 shard_map.75.front_in
  378.9 1.0 collective-permute-done.tiles
  379.8 1.3 shard_map.76
Async XLA Ops:
  8.2 112.4 %collective-permute-start.8 = (f32[32,128,128]{2,1,0:T(8,128)S(1)}, f32[32,128,128]{2,1,0:T(8,128)S(1)}, u32[]{:S(2)}, u32[]{:S(2)}) collective-permute-start(f32[32,128,128]{2,1,0:T(8,128)S(1)} %shard_map.63), channel_id=1, source_target_pairs={{0,1},{1,0},{2,3},{3,2},{4,5},{5,4},{6,7},{7,6},{8,9},{9,8},{10,11... | collective-permute-start | bytes 6291464 | tf_op jit(solution)/shard_map/ppermute | solution.py:307
  15.7 92.2 %collective-permute-start.5 = (f32[24,128,128]{2,1,0:T(8,128)S(1)}, f32[24,128,128]{2,1,0:T(8,128)S(1)}, u32[]{:S(2)}, u32[]{:S(2)}) collective-permute-start(f32[24,128,128]{2,1,0:T(8,128)S(1)} %shard_map.60), channel_id=1, source_target_pairs={{0,6},{1,7},{2,4},{3,5},{4,2},{5,3},{6,0},{7,1},{8,14},{9,15},{10,... | collective-permute-start | bytes 4718600 | tf_op jit(solution)/shard_map/ppermute | solution.py:307
  19.3 80.2 %collective-permute-start.7 = (f32[2,128,128]{2,1,0:T(8,128)S(1)}, f32[2,128,128]{2,1,0:T(8,128)S(1)}, u32[]{:S(2)}, u32[]{:S(2)}) collective-permute-start(f32[2,128,128]{2,1,0:T(8,128)S(1)} %shard_map.62), channel_id=1, source_target_pairs={{0,6},{1,7},{2,4},{3,5},{4,2},{5,3},{6,0},{7,1},{8,14},{9,15},{10,... | collective-permute-start | bytes 393224 | tf_op jit(solution)/shard_map/ppermute | solution.py:307
  23.8 84.0 %collective-permute-start.6 = (f32[6,128,128]{2,1,0:T(8,128)S(1)}, f32[6,128,128]{2,1,0:T(8,128)S(1)}, u32[]{:S(2)}, u32[]{:S(2)}) collective-permute-start(f32[6,128,128]{2,1,0:T(8,128)S(1)} %shard_map.61), channel_id=1, source_target_pairs={{0,6},{1,7},{2,4},{3,5},{4,2},{5,3},{6,0},{7,1},{8,14},{9,15},{10,... | collective-permute-start | bytes 1179656 | tf_op jit(solution)/shard_map/ppermute | solution.py:307
  33.4 90.5 %collective-permute-start.4 = (f32[32,128,128]{2,1,0:T(8,128)S(1)}, f32[32,128,128]{2,1,0:T(8,128)S(1)}, u32[]{:S(2)}, u32[]{:S(2)}) collective-permute-start(f32[32,128,128]{2,1,0:T(8,128)S(1)} %shard_map.59), channel_id=1, source_target_pairs={{0,2},{1,3},{2,0},{3,1},{4,6},{5,7},{6,4},{7,5},{8,10},{9,11},{10,... | collective-permute-start | bytes 6291464 | tf_op jit(solution)/shard_map/ppermute | solution.py:307
  99.4 97.6 %collective-permute-start.3 = (f32[32,128,128]{2,1,0:T(8,128)S(1)}, f32[32,128,128]{2,1,0:T(8,128)S(1)}, u32[]{:S(2)}, u32[]{:S(2)}) collective-permute-start(f32[32,128,128]{2,1,0:T(8,128)S(1)} %shard_map.58), channel_id=1, source_target_pairs={{0,3},{1,2},{2,1},{3,0},{4,7},{5,6},{6,5},{7,4},{8,11},{9,10},{10,... | collective-permute-start | bytes 6291464 | tf_op jit(solution)/shard_map/ppermute | solution.py:307
  107.9 92.7 %collective-permute-start.2 = (f32[32,128,128]{2,1,0:T(8,128)S(1)}, f32[32,128,128]{2,1,0:T(8,128)S(1)}, u32[]{:S(2)}, u32[]{:S(2)}) collective-permute-start(f32[32,128,128]{2,1,0:T(8,128)S(1)} %shard_map.57), channel_id=1, source_target_pairs={{0,4},{1,5},{2,6},{3,7},{4,0},{5,1},{6,2},{7,3},{8,12},{9,13},{10,... | collective-permute-start | bytes 6291464 | tf_op jit(solution)/shard_map/ppermute | solution.py:307
  107.9 224.2 %collective-permute-start.1 = (f32[32,128,128]{2,1,0:T(8,128)S(1)}, f32[32,128,128]{2,1,0:T(8,128)S(1)}, u32[]{:S(2)}, u32[]{:S(2)}) collective-permute-start(f32[32,128,128]{2,1,0:T(8,128)S(1)} %shard_map.56), channel_id=1, source_target_pairs={{0,5},{1,4},{2,7},{3,6},{4,1},{5,0},{6,3},{7,2},{8,13},{9,12},{10,... | collective-permute-start | bytes 6291464 | tf_op jit(solution)/shard_map/ppermute | solution.py:307
  120.6 254.9 %collective-permute-start.9 = (f32[28,128,128]{2,1,0:T(8,128)S(1)}, f32[28,128,128]{2,1,0:T(8,128)S(1)}, u32[]{:S(2)}, u32[]{:S(2)}) collective-permute-start(f32[28,128,128]{2,1,0:T(8,128)S(1)} %shard_map.74), channel_id=1, source_target_pairs={{0,7},{1,6},{2,5},{3,4},{4,3},{5,2},{6,1},{7,0},{8,15},{9,14},{10,... | collective-permute-start | bytes 5505032 | tf_op jit(solution)/shard_map/ppermute | solution.py:307
  123.9 41.5 %copy-start = (s32[2,32]{1,0:T(2,128)S(1)}, s32[2,32]{1,0:T(2,128)}, u32[]{:S(2)}) copy-start(s32[2,32]{1,0:T(2,128)} %labels.43) | copy-start | bytes 772
  123.9 255.9 %collective-permute-start = (f32[4,128,128]{2,1,0:T(8,128)S(1)}, f32[4,128,128]{2,1,0:T(8,128)S(1)}, u32[]{:S(2)}, u32[]{:S(2)}) collective-permute-start(f32[4,128,128]{2,1,0:T(8,128)S(1)} %shard_map.55), channel_id=1, source_target_pairs={{0,7},{1,6},{2,5},{3,4},{4,3},{5,2},{6,1},{7,0},{8,15},{9,14},{10,... | collective-permute-start | bytes 786440 | tf_op jit(solution)/shard_map/ppermute | solution.py:307
